TPU v7x, 32 devices: a whole 2x2x4 slice. The times are simulated.
32 devices in a mesh: gx: 4 (over y, x), gy: 8 (over z, core).
Axes of the slice: x: 2, y: 2, z: 4, core: 2. Of those that a mesh axis runs over, the one named last changes fastest.
Arguments:
- position: float32 [2, 24, 48, 128], P(None, 'gx', 'gy'), may hold values from 0 to 1
- velocity: float32 [2, 24, 48, 128], P(None, 'gx', 'gy'), may hold values from -3 to 3
- other_accel: float32 [2, 24, 48, 128], P(None, 'gx', 'gy'), may hold values from -5 to 5
- phase_ids: int32 [24, 48, 128], P('gx', 'gy'), may hold values from 0 to 1, as said below
- counts: int32 [24, 48], P('gx', 'gy'), may hold values from 48 to 128, as said below
Outputs:
- new_position: float32 [2, 24, 48, 128], P(None, 'gx', 'gy')
- new_velocity: float32 [2, 24, 48, 128], P(None, 'gx', 'gy')
- pressure: float32 [24, 48, 128], P('gx', 'gy')
- monitor: float32 [4, 4], replicated
Inputs may be any that keep to these rules, and one draw needn't show every extreme that they name: `counts`: each entry is the number of live slots of its cell; the live slots are the first ones of the cell; some cell holds 128. `phase_ids`: both phases occur among the live slots.
All inputs are finite; a program needn't handle non-finite values.
Results may differ from a plain program's by a relative error of at most 0.0001.
Values sent between devices are 32-bit elements; how exact they have to be, the bound alone decides.
A program may use at most 64 MiB of HBM per device.

v0:
```python
import jax
import jax.numpy as jnp
from jax import lax
from jax.sharding import PartitionSpec as P

ITERS = 4


TIME_STEP = 0.05
KERNEL_NORM = 4.0 / (3.141592653589793 * 64.0)
REST_LIGHT = 1.2
REST_HEAVY = 1.5
STIFF_LIGHT = 100.0
STIFF_HEAVY = 200.0
MASS_LIGHT = 1.0
MASS_HEAVY = 1.5
SENTINEL = 1e30


def padded(block, sides, width):
    for axis, dim in sides:
        count = lax.axis_size(axis)
        forward = [(i, i + 1) for i in range(count - 1)]
        forward.append((count - 1, 0))
        backward = [(target, source) for source, target in forward]
        low = lax.ppermute(
            lax.slice_in_dim(block, block.shape[dim] - width, None, axis=dim), axis, forward
        )
        high = lax.ppermute(lax.slice_in_dim(block, 0, width, axis=dim), axis, backward)
        block = jnp.concatenate([low, block, high], axis=dim)
    return block


def window_of(source, off_x, off_y, row_count, col_count):
    return source[1 + off_x : 1 + off_x + row_count, 1 + off_y : 1 + off_y + col_count]


def pair_sums(centers, padded_list, with_force):
    center_x, center_y = (centers[0], centers[1])
    near_x, near_y, near_live = (padded_list[0], padded_list[1], padded_list[2])
    row_count, col_count = (center_x.shape[0], center_x.shape[1])
    total_a = jnp.zeros_like(center_x)
    total_b = jnp.zeros_like(center_x)
    for off_x in (-1, 0, 1):
        for off_y in (-1, 0, 1):
            other_x = window_of(near_x, off_x, off_y, row_count, col_count)
            other_y = window_of(near_y, off_x, off_y, row_count, col_count)
            other_live = window_of(near_live, off_x, off_y, row_count, col_count)
            diff_x = center_x[..., :, None] - (other_x[..., None, :] + off_x)
            diff_y = center_y[..., :, None] - (other_y[..., None, :] + off_y)
            intersection = (
                jnp.maximum(1.0 - diff_x * diff_x - diff_y * diff_y, 0.0) * other_live[..., None, :]
            )
            if with_force:
                other_term = window_of(padded_list[3], off_x, off_y, row_count, col_count)
                pair_coef = (
                    intersection
                    * intersection
                    * (centers[2][..., :, None] + other_term[..., None, :])
                )
                total_a = total_a + jnp.sum(pair_coef * diff_x, axis=-1)
                total_b = total_b + jnp.sum(pair_coef * diff_y, axis=-1)
            else:
                total_a = total_a + jnp.sum(intersection * intersection * intersection, axis=-1)
    if with_force:
        return (total_a, total_b)
    return (total_a,)


def blocked(with_force, centers, padded_list, row_count):
    block_count = row_count // 2

    def one_block(block_index):
        first_row = block_index * 2
        center_part = tuple(
            (lax.dynamic_slice_in_dim(source, first_row, 2, 0) for source in centers)
        )
        padded_part = tuple(
            (lax.dynamic_slice_in_dim(source, first_row, 4, 0) for source in padded_list)
        )
        return pair_sums(center_part, padded_part, with_force)

    results = lax.map(one_block, jnp.arange(block_count, dtype=jnp.int32))
    return tuple((source.reshape((row_count,) + source.shape[2:]) for source in results))


def global_bounds(density_ratio, live_bool, heavy_bool):
    light_sel = live_bool & jnp.logical_not(heavy_bool)
    heavy_sel = live_bool & heavy_bool
    top_local = jnp.stack(
        [
            jnp.max(jnp.where(light_sel, density_ratio, -SENTINEL)),
            jnp.max(jnp.where(heavy_sel, density_ratio, -SENTINEL)),
        ]
    )
    low_local = jnp.stack(
        [
            jnp.min(jnp.where(light_sel, density_ratio, SENTINEL)),
            jnp.min(jnp.where(heavy_sel, density_ratio, SENTINEL)),
        ]
    )
    bounds = lax.pmax(jnp.concatenate([top_local, -low_local]), ("gx", "gy"))
    top_ratio = bounds[:2]
    low_ratio = -bounds[2:]
    return (top_ratio, low_ratio)


def phase_params(heavy_bool):
    rest_density = jnp.where(heavy_bool, REST_HEAVY, REST_LIGHT).astype(jnp.float32)
    stiffness = jnp.where(heavy_bool, STIFF_HEAVY, STIFF_LIGHT).astype(jnp.float32)
    return (rest_density, stiffness)


def pressure_update(pressure, density_sum, live_bool, heavy_bool, own_live, own_heavy):
    live_mask = live_bool.astype(jnp.float32)
    rest_density, stiffness = phase_params(heavy_bool)
    density = KERNEL_NORM * density_sum
    density_ratio = density / rest_density
    top_ratio, low_ratio = global_bounds(density_ratio, own_live, own_heavy)
    relaxation = 1.0 / (1.0 + top_ratio - low_ratio)
    particle_relax = jnp.where(heavy_bool, relaxation[1], relaxation[0])
    pressure = live_mask * (pressure + stiffness * particle_relax * (density_ratio - 1.0))
    safe_density = jnp.where(live_bool, density, 1.0)
    press_term = jnp.where(live_bool, pressure / (safe_density * safe_density), 0.0)
    return (pressure, press_term, jnp.concatenate([top_ratio, low_ratio]))


def local(position, velocity, other_accel, phase_ids, counts):
    tile_rows, tile_cols, slot_count = phase_ids.shape
    slot_index = jnp.arange(slot_count, dtype=jnp.int32)
    live_bool = slot_index[None, None, :] < counts[:, :, None]
    heavy_bool = phase_ids == 1
    live_mask = live_bool.astype(jnp.float32)
    particle_mass = jnp.where(heavy_bool, MASS_HEAVY, MASS_LIGHT).astype(jnp.float32)
    slot_codes = jnp.where(live_bool, phase_ids + 1, 0)
    padded_codes = padded(slot_codes, (("gx", 0), ("gy", 1)), 2)
    cycle_codes = padded_codes[1:-1, 1:-1]
    cycle_live = cycle_codes > 0
    cycle_mask = cycle_live.astype(jnp.float32)
    accel_x = jnp.zeros_like(live_mask)
    accel_y = jnp.zeros_like(live_mask)
    monitor_rows = []
    pressure = jnp.zeros_like(live_mask)
    for iteration in range(ITERS):
        vel_x = velocity[0] + TIME_STEP * (other_accel[0] + accel_x)
        vel_y = velocity[1] + TIME_STEP * (other_accel[1] + accel_y)
        pos_x = position[0] + TIME_STEP * vel_x
        pos_y = position[1] + TIME_STEP * vel_y
        moved = padded(jnp.stack([pos_x, pos_y]), (("gx", 1), ("gy", 2)), 1)
        (density_sum,) = blocked(False, (pos_x, pos_y), (moved[0], moved[1], cycle_mask), tile_rows)
        pressure, press_term, monitor_row = pressure_update(
            pressure, density_sum, live_bool, heavy_bool, live_bool, heavy_bool
        )
        near_term = padded(press_term, (("gx", 0), ("gy", 1)), 1)
        force_x, force_y = blocked(
            True, (pos_x, pos_y, press_term), (moved[0], moved[1], cycle_mask, near_term), tile_rows
        )
        accel_x = live_mask * (6.0 * KERNEL_NORM / particle_mass) * force_x
        accel_y = live_mask * (6.0 * KERNEL_NORM / particle_mass) * force_y
        monitor_rows.append(monitor_row)
    new_vel_x = live_mask * (velocity[0] + TIME_STEP * (other_accel[0] + accel_x))
    new_vel_y = live_mask * (velocity[1] + TIME_STEP * (other_accel[1] + accel_y))
    new_pos_x = live_mask * (position[0] + TIME_STEP * new_vel_x)
    new_pos_y = live_mask * (position[1] + TIME_STEP * new_vel_y)
    return (
        jnp.stack([new_pos_x, new_pos_y]),
        jnp.stack([new_vel_x, new_vel_y]),
        pressure,
        jnp.stack(monitor_rows),
    )


def solution(mesh):
    placed = (
        P(None, "gx", "gy", None),
        P(None, "gx", "gy", None),
        P(None, "gx", "gy", None),
        P("gx", "gy", None),
        P("gx", "gy"),
    )
    return jax.shard_map(
        local,
        mesh=mesh,
        in_specs=placed,
        out_specs=(P(None, "gx", "gy", None), P(None, "gx", "gy", None), P("gx", "gy", None), P()),
        check_vma=False,
    )
```

profile of v0, /device:TPU:0, one launch (start us, length us, event | category | flops | bytes accessed | tf_op | source)
XLA Modules:
  0.0 452.7 jit_solution(12311317987934196679)
XLA Ops:
  9.6 3.5 collective-permute-start.3
  13.2 3.5 collective-permute-start.7
  18.2 16.3 %while.88 = (s32[]{:T(128)}, f32[3,2,6,128]{3,2,1,0:T(8,128)S(1)}, s32[3]{0:T(128)S(1)}, f32[6,6,128]{2,1,0:T(8,128)S(1)}, f32[8,8,128]{2,1,0:T(8,128)S(1)}, /*i...) while((s32[]{:T(128)}, f32[3,2,6,128]{3,2,1,0:T(8,128)S(1)}, ...), condition=%wide.region_10.11_spmd, body=%wide.region_0.10_spmd.sunk | while | flops 19481100 | bytes 684356 | solution.py:83
  37.9 39.1 %pmax.28 = f32[4]{0:T(128)S(1)} all-reduce(f32[4]{0:T(128)S(1)} %pad_maximum_fusion.47), channel_id=1, replica_groups=mesh['gx'=4,'gy'=8] {'gx','gy'}, use_global_device_ids=true, to_apply=%region_15.16 | all-reduce | flops 4 | bytes 32 | tf_op jit(solution)/shard_map/pmax | solution.py:102
  85.1 3.5 collective-permute-start.11
  90.0 26.8 %while.89 = (s32[]{:T(128)}, f32[3,2,6,128]{3,2,1,0:T(8,128)S(1)}, f32[3,2,6,128]{3,2,1,0:T(8,128)S(1)}, s32[3]{0:T(128)S(1)}, f32[6,6,128]{2,1,0:T(8,128)S(1)},...) while((s32[]{:T(128)}, f32[3,2,6,128]{3,2,1,0:T(8,128)S(1)}, ...), condition=%wide.region_35.36_spmd, body=%wide.region_16.35_spmd.sunk | while | flops 26557452 | bytes 1030516 | solution.py:83
  95.8 3.1 fusion.506
  104.7 3.1 fusion.506
  113.7 3.1 fusion.506
  123.1 3.5 collective-permute-start.15
  128.1 16.3 %while.90 = (s32[]{:T(128)}, f32[3,2,6,128]{3,2,1,0:T(8,128)S(1)}, s32[3]{0:T(128)S(1)}, f32[6,6,128]{2,1,0:T(8,128)S(1)}, f32[8,8,128]{2,1,0:T(8,128)S(1)}, /*i...) while((s32[]{:T(128)}, f32[3,2,6,128]{3,2,1,0:T(8,128)S(1)}, ...), condition=%wide.region_46.47_spmd, body=%wide.region_36.46_spmd.sunk | while | flops 19481100 | bytes 684356 | solution.py:83
  147.7 38.1 %pmax.29 = f32[4]{0:T(128)S(1)} all-reduce(f32[4]{0:T(128)S(1)} %pad_maximum_fusion.48), channel_id=1, replica_groups=mesh['gx'=4,'gy'=8] {'gx','gy'}, use_global_device_ids=true, to_apply=%region_51.52 | all-reduce | flops 4 | bytes 32 | tf_op jit(solution)/shard_map/pmax | solution.py:102
  195.1 3.5 collective-permute-start.19
  200.0 26.8 %while.91 = (s32[]{:T(128)}, f32[3,2,6,128]{3,2,1,0:T(8,128)S(1)}, f32[3,2,6,128]{3,2,1,0:T(8,128)S(1)}, s32[3]{0:T(128)S(1)}, f32[6,6,128]{2,1,0:T(8,128)S(1)},...) while((s32[]{:T(128)}, f32[3,2,6,128]{3,2,1,0:T(8,128)S(1)}, ...), condition=%wide.region_71.72_spmd, body=%wide.region_52.71_spmd.sunk | while | flops 26557452 | bytes 1030516 | solution.py:83
  205.8 3.1 fusion.513
  214.7 3.1 fusion.513
  233.1 3.5 collective-permute-start.23
  238.0 16.3 %while.92 = (s32[]{:T(128)}, f32[3,2,6,128]{3,2,1,0:T(8,128)S(1)}, s32[3]{0:T(128)S(1)}, f32[6,6,128]{2,1,0:T(8,128)S(1)}, f32[8,8,128]{2,1,0:T(8,128)S(1)}, /*i...) while((s32[]{:T(128)}, f32[3,2,6,128]{3,2,1,0:T(8,128)S(1)}, ...), condition=%wide.region_82.83_spmd, body=%wide.region_72.82_spmd.sunk | while | flops 19481100 | bytes 684356 | solution.py:83
  257.8 38.2 %pmax.30 = f32[4]{0:T(128)S(1)} all-reduce(f32[4]{0:T(128)S(1)} %pad_maximum_fusion.49), channel_id=1, replica_groups=mesh['gx'=4,'gy'=8] {'gx','gy'}, use_global_device_ids=true, to_apply=%region_87.88 | all-reduce | flops 4 | bytes 32 | tf_op jit(solution)/shard_map/pmax | solution.py:102
  296.7 3.8 fusion.444
  306.6 3.5 collective-permute-start.27
  311.5 26.8 %while.93 = (s32[]{:T(128)}, f32[3,2,6,128]{3,2,1,0:T(8,128)S(1)}, f32[3,2,6,128]{3,2,1,0:T(8,128)S(1)}, s32[3]{0:T(128)S(1)}, f32[6,6,128]{2,1,0:T(8,128)S(1)},...) while((s32[]{:T(128)}, f32[3,2,6,128]{3,2,1,0:T(8,128)S(1)}, ...), condition=%wide.region_107.108_spmd, body=%wide.region_88.107_spmd.sunk | while | flops 26557452 | bytes 1030516 | solution.py:83
  326.2 3.1 fusion.520
  344.5 3.5 collective-permute-start.31
  349.5 16.3 %while.94 = (s32[]{:T(128)}, f32[3,2,6,128]{3,2,1,0:T(8,128)S(1)}, s32[3]{0:T(128)S(1)}, f32[6,6,128]{2,1,0:T(8,128)S(1)}, f32[8,8,128]{2,1,0:T(8,128)S(1)}, /*i...) while((s32[]{:T(128)}, f32[3,2,6,128]{3,2,1,0:T(8,128)S(1)}, ...), condition=%wide.region_118.119_spmd, body=%wide.region_108.118_spmd.sunk | while | flops 19481100 | bytes 684356 | solution.py:83
  369.1 38.1 %pmax.31 = f32[4]{0:T(128)S(1)} all-reduce(f32[4]{0:T(128)S(1)} %pad_maximum_fusion.50), channel_id=1, replica_groups=mesh['gx'=4,'gy'=8] {'gx','gy'}, use_global_device_ids=true, to_apply=%region_123.124 | all-reduce | flops 4 | bytes 32 | tf_op jit(solution)/shard_map/pmax | solution.py:102
  407.9 5.7 %fusion.441 = (f32[6,6,128]{2,1,0:T(8,128)S(1)}, f32[6,6,128]{2,1,0:T(8,128)}) fusion(f32[3,2,6,128]{3,2,1,0:T(8,128)S(1)} %broadcast_multiply_fusion, s32[6,6]{1,0:T(8,128)S(1)} %copy-done, pred[6,6,128]{2,1,0:T(8,128)(4,1)S(1)} %get-tuple-element.764, f32[]{:T(128)} %bitcast.73, f32[]{:T(128)} %bitcast.72, ...), kind=kLoop, calls=%fused_computation.950 | loop fusion | flops 156672 | bytes 115376 | tf_op jit(solution)/shard_map/jit(_where)/select_n | solution.py:124
  419.6 3.5 collective-permute-start.35
  424.5 26.8 %while.95 = (s32[]{:T(128)}, f32[3,2,6,128]{3,2,1,0:T(8,128)S(1)}, f32[3,2,6,128]{3,2,1,0:T(8,128)S(1)}, s32[3]{0:T(128)S(1)}, f32[6,6,128]{2,1,0:T(8,128)S(1)},...) while((s32[]{:T(128)}, f32[3,2,6,128]{3,2,1,0:T(8,128)S(1)}, ...), condition=%wide.region_143.144_spmd, body=%wide.region_124.143_spmd.sunk | while | flops 26557452 | bytes 1030516 | solution.py:83
  427.2 3.1 fusion.528
  436.1 3.1 fusion.528
  445.0 3.1 fusion.528
  (362 shorter events, 210.9 us)
Async XLA Ops:
  2.4 7.1 %collective-permute-start = (f32[2,1,6,128]{3,2,1,0:T(8,128)S(1)}, f32[2,1,6,128]{3,2,1,0:T(8,128)S(1)}, u32[]{:S(2)}, u32[]{:S(2)}) collective-permute-start(f32[2,1,6,128]{3,2,1,0:T(8,128)S(1)} %get-tuple-element.1127), channel_id=1, source_target_pairs={{0,8},{8,16},{16,24},{24,0},{1,9},{9,17},{17,25},{25,1},{2,10},{10... | collective-permute-start | bytes 18440 | tf_op jit(solution)/shard_map/ppermute | solution.py:26
  5.4 4.1 collective-permute-start.1
  6.5 6.6 %collective-permute-start.4 = (s32[2,6,128]{2,1,0:T(8,128)S(1)}, s32[2,6,128]{2,1,0:T(8,128)S(1)}, u32[]{:S(2)}, u32[]{:S(2)}) collective-permute-start(s32[2,6,128]{2,1,0:T(8,128)S(1)} %get-tuple-element.1153), channel_id=1, source_target_pairs={{0,8},{8,16},{16,24},{24,0},{1,9},{9,17},{17,25},{25,1},{2,10},{10... | collective-permute-start | bytes 18440 | tf_op jit(solution)/shard_map/ppermute | solution.py:26
  7.6 5.6 %collective-permute-start.5 = (s32[2,6,128]{2,1,0:T(8,128)S(1)}, s32[2,6,128]{2,1,0:T(8,128)S(1)}, u32[]{:S(2)}, u32[]{:S(2)}) collective-permute-start(s32[2,6,128]{2,1,0:T(8,128)S(1)} %get-tuple-element.1154), channel_id=1, source_target_pairs={{8,0},{16,8},{24,16},{0,24},{9,1},{17,9},{25,17},{1,25},{10,2},{18... | collective-permute-start | bytes 18440 | tf_op jit(solution)/shard_map/ppermute | solution.py:29
  9.5 7.2 %collective-permute-start.2 = (f32[2,8,1,128]{3,2,1,0:T(1,128)S(1)}, f32[2,8,1,128]{3,2,1,0:T(1,128)S(1)}, u32[]{:S(2)}, u32[]{:S(2)}) collective-permute-start(f32[2,8,1,128]{3,2,1,0:T(1,128)S(1)} %get-tuple-element.1119), channel_id=1, source_target_pairs={{0,1},{1,2},{2,3},{3,4},{4,5},{5,6},{6,7},{7,0},{8,9},{9,10},{10,1... | collective-permute-start | bytes 24584 | tf_op jit(solution)/shard_map/ppermute | solution.py:26
  9.6 7.2 %collective-permute-start.3 = (f32[2,8,1,128]{3,2,1,0:T(1,128)S(1)}, f32[2,8,1,128]{3,2,1,0:T(1,128)S(1)}, u32[]{:S(2)}, u32[]{:S(2)}) collective-permute-start(f32[2,8,1,128]{3,2,1,0:T(1,128)S(1)} %get-tuple-element.1120), channel_id=1, source_target_pairs={{1,0},{2,1},{3,2},{4,3},{5,4},{6,5},{7,6},{0,7},{9,8},{10,9},{11,1... | collective-permute-start | bytes 24584 | tf_op jit(solution)/shard_map/ppermute | solution.py:29
  13.2 4.9 %collective-permute-start.6 = (s32[10,2,128]{2,1,0:T(2,128)S(1)}, s32[10,2,128]{2,1,0:T(2,128)S(1)}, u32[]{:S(2)}, u32[]{:S(2)}) collective-permute-start(s32[10,2,128]{2,1,0:T(2,128)S(1)} %get-tuple-element.1129), channel_id=1, source_target_pairs={{0,1},{1,2},{2,3},{3,4},{4,5},{5,6},{6,7},{7,0},{8,9},{9,10},{10,1... | collective-permute-start | bytes 30728 | tf_op jit(solution)/shard_map/ppermute | solution.py:26
  13.2 4.9 %collective-permute-start.7 = (s32[10,2,128]{2,1,0:T(2,128)S(1)}, s32[10,2,128]{2,1,0:T(2,128)S(1)}, u32[]{:S(2)}, u32[]{:S(2)}) collective-permute-start(s32[10,2,128]{2,1,0:T(2,128)S(1)} %get-tuple-element.1130), channel_id=1, source_target_pairs={{1,0},{2,1},{3,2},{4,3},{5,4},{6,5},{7,6},{0,7},{9,8},{10,9},{11,1... | collective-permute-start | bytes 30728 | tf_op jit(solution)/shard_map/ppermute | solution.py:29
  79.1 4.6 %collective-permute-start.8 = (f32[1,6,128]{2,1,0:T(8,128)S(1)}, f32[1,6,128]{2,1,0:T(8,128)S(1)}, u32[]{:S(2)}, u32[]{:S(2)}) collective-permute-start(f32[1,6,128]{2,1,0:T(8,128)S(1)} %get-tuple-element.1151), channel_id=1, source_target_pairs={{0,8},{8,16},{16,24},{24,0},{1,9},{9,17},{17,25},{25,1},{2,10},{10... | collective-permute-start | bytes 9224 | tf_op jit(solution)/shard_map/ppermute | solution.py:26
  85.1 4.9 %collective-permute-start.10 = (f32[8,1,128]{2,1,0:T(1,128)S(1)}, f32[8,1,128]{2,1,0:T(1,128)S(1)}, u32[]{:S(2)}, u32[]{:S(2)}) collective-permute-start(f32[8,1,128]{2,1,0:T(1,128)S(1)} %get-tuple-element.1143), channel_id=1, source_target_pairs={{0,1},{1,2},{2,3},{3,4},{4,5},{5,6},{6,7},{7,0},{8,9},{9,10},{10,1... | collective-permute-start | bytes 12296 | tf_op jit(solution)/shard_map/ppermute | solution.py:26
  85.1 4.9 %collective-permute-start.11 = (f32[8,1,128]{2,1,0:T(1,128)S(1)}, f32[8,1,128]{2,1,0:T(1,128)S(1)}, u32[]{:S(2)}, u32[]{:S(2)}) collective-permute-start(f32[8,1,128]{2,1,0:T(1,128)S(1)} %get-tuple-element.1144), channel_id=1, source_target_pairs={{1,0},{2,1},{3,2},{4,3},{5,4},{6,5},{7,6},{0,7},{9,8},{10,9},{11,1... | collective-permute-start | bytes 12296 | tf_op jit(solution)/shard_map/ppermute | solution.py:29
  117.0 4.6 %collective-permute-start.12 = (f32[2,1,6,128]{3,2,1,0:T(8,128)S(1)}, f32[2,1,6,128]{3,2,1,0:T(8,128)S(1)}, u32[]{:S(2)}, u32[]{:S(2)}) collective-permute-start(f32[2,1,6,128]{3,2,1,0:T(8,128)S(1)} %get-tuple-element.1125), channel_id=1, source_target_pairs={{0,8},{8,16},{16,24},{24,0},{1,9},{9,17},{17,25},{25,1},{2,10},{10... | collective-permute-start | bytes 18440 | tf_op jit(solution)/shard_map/ppermute | solution.py:26
  119.4 3.7 collective-permute-start.13
  123.0 4.9 %collective-permute-start.14 = (f32[2,8,1,128]{3,2,1,0:T(1,128)S(1)}, f32[2,8,1,128]{3,2,1,0:T(1,128)S(1)}, u32[]{:S(2)}, u32[]{:S(2)}) collective-permute-start(f32[2,8,1,128]{3,2,1,0:T(1,128)S(1)} %get-tuple-element.1115), channel_id=1, source_target_pairs={{0,1},{1,2},{2,3},{3,4},{4,5},{5,6},{6,7},{7,0},{8,9},{9,10},{10,1... | collective-permute-start | bytes 24584 | tf_op jit(solution)/shard_map/ppermute | solution.py:26
  123.1 4.9 %collective-permute-start.15 = (f32[2,8,1,128]{3,2,1,0:T(1,128)S(1)}, f32[2,8,1,128]{3,2,1,0:T(1,128)S(1)}, u32[]{:S(2)}, u32[]{:S(2)}) collective-permute-start(f32[2,8,1,128]{3,2,1,0:T(1,128)S(1)} %get-tuple-element.1116), channel_id=1, source_target_pairs={{1,0},{2,1},{3,2},{4,3},{5,4},{6,5},{7,6},{0,7},{9,8},{10,9},{11,1... | collective-permute-start | bytes 24584 | tf_op jit(solution)/shard_map/ppermute | solution.py:29
  189.1 4.6 %collective-permute-start.16 = (f32[1,6,128]{2,1,0:T(8,128)S(1)}, f32[1,6,128]{2,1,0:T(8,128)S(1)}, u32[]{:S(2)}, u32[]{:S(2)}) collective-permute-start(f32[1,6,128]{2,1,0:T(8,128)S(1)} %get-tuple-element.1149), channel_id=1, source_target_pairs={{0,8},{8,16},{16,24},{24,0},{1,9},{9,17},{17,25},{25,1},{2,10},{10... | collective-permute-start | bytes 9224 | tf_op jit(solution)/shard_map/ppermute | solution.py:26
  195.0 4.9 %collective-permute-start.18 = (f32[8,1,128]{2,1,0:T(1,128)S(1)}, f32[8,1,128]{2,1,0:T(1,128)S(1)}, u32[]{:S(2)}, u32[]{:S(2)}) collective-permute-start(f32[8,1,128]{2,1,0:T(1,128)S(1)} %get-tuple-element.1141), channel_id=1, source_target_pairs={{0,1},{1,2},{2,3},{3,4},{4,5},{5,6},{6,7},{7,0},{8,9},{9,10},{10,1... | collective-permute-start | bytes 12296 | tf_op jit(solution)/shard_map/ppermute | solution.py:26
  195.1 4.9 %collective-permute-start.19 = (f32[8,1,128]{2,1,0:T(1,128)S(1)}, f32[8,1,128]{2,1,0:T(1,128)S(1)}, u32[]{:S(2)}, u32[]{:S(2)}) collective-permute-start(f32[8,1,128]{2,1,0:T(1,128)S(1)} %get-tuple-element.1142), channel_id=1, source_target_pairs={{1,0},{2,1},{3,2},{4,3},{5,4},{6,5},{7,6},{0,7},{9,8},{10,9},{11,1... | collective-permute-start | bytes 12296 | tf_op jit(solution)/shard_map/ppermute | solution.py:29
  226.9 4.6 %collective-permute-start.20 = (f32[2,1,6,128]{3,2,1,0:T(8,128)S(1)}, f32[2,1,6,128]{3,2,1,0:T(8,128)S(1)}, u32[]{:S(2)}, u32[]{:S(2)}) collective-permute-start(f32[2,1,6,128]{3,2,1,0:T(8,128)S(1)} %get-tuple-element.1123), channel_id=1, source_target_pairs={{0,8},{8,16},{16,24},{24,0},{1,9},{9,17},{17,25},{25,1},{2,10},{10... | collective-permute-start | bytes 18440 | tf_op jit(solution)/shard_map/ppermute | solution.py:26
  229.3 3.7 collective-permute-start.21
  233.0 4.9 %collective-permute-start.22 = (f32[2,8,1,128]{3,2,1,0:T(1,128)S(1)}, f32[2,8,1,128]{3,2,1,0:T(1,128)S(1)}, u32[]{:S(2)}, u32[]{:S(2)}) collective-permute-start(f32[2,8,1,128]{3,2,1,0:T(1,128)S(1)} %get-tuple-element.1111), channel_id=1, source_target_pairs={{0,1},{1,2},{2,3},{3,4},{4,5},{5,6},{6,7},{7,0},{8,9},{9,10},{10,1... | collective-permute-start | bytes 24584 | tf_op jit(solution)/shard_map/ppermute | solution.py:26
  233.1 4.9 %collective-permute-start.23 = (f32[2,8,1,128]{3,2,1,0:T(1,128)S(1)}, f32[2,8,1,128]{3,2,1,0:T(1,128)S(1)}, u32[]{:S(2)}, u32[]{:S(2)}) collective-permute-start(f32[2,8,1,128]{3,2,1,0:T(1,128)S(1)} %get-tuple-element.1112), channel_id=1, source_target_pairs={{1,0},{2,1},{3,2},{4,3},{5,4},{6,5},{7,6},{0,7},{9,8},{10,9},{11,1... | collective-permute-start | bytes 24584 | tf_op jit(solution)/shard_map/ppermute | solution.py:29
  300.6 4.6 %collective-permute-start.24 = (f32[1,6,128]{2,1,0:T(8,128)S(1)}, f32[1,6,128]{2,1,0:T(8,128)S(1)}, u32[]{:S(2)}, u32[]{:S(2)}) collective-permute-start(f32[1,6,128]{2,1,0:T(8,128)S(1)} %get-tuple-element.1147), channel_id=1, source_target_pairs={{0,8},{8,16},{16,24},{24,0},{1,9},{9,17},{17,25},{25,1},{2,10},{10... | collective-permute-start | bytes 9224 | tf_op jit(solution)/shard_map/ppermute | solution.py:26
  306.5 4.9 %collective-permute-start.26 = (f32[8,1,128]{2,1,0:T(1,128)S(1)}, f32[8,1,128]{2,1,0:T(1,128)S(1)}, u32[]{:S(2)}, u32[]{:S(2)}) collective-permute-start(f32[8,1,128]{2,1,0:T(1,128)S(1)} %get-tuple-element.1139), channel_id=1, source_target_pairs={{0,1},{1,2},{2,3},{3,4},{4,5},{5,6},{6,7},{7,0},{8,9},{9,10},{10,1... | collective-permute-start | bytes 12296 | tf_op jit(solution)/shard_map/ppermute | solution.py:26
  306.6 4.9 %collective-permute-start.27 = (f32[8,1,128]{2,1,0:T(1,128)S(1)}, f32[8,1,128]{2,1,0:T(1,128)S(1)}, u32[]{:S(2)}, u32[]{:S(2)}) collective-permute-start(f32[8,1,128]{2,1,0:T(1,128)S(1)} %get-tuple-element.1140), channel_id=1, source_target_pairs={{1,0},{2,1},{3,2},{4,3},{5,4},{6,5},{7,6},{0,7},{9,8},{10,9},{11,1... | collective-permute-start | bytes 12296 | tf_op jit(solution)/shard_map/ppermute | solution.py:29
  338.4 4.6 %collective-permute-start.28 = (f32[2,1,6,128]{3,2,1,0:T(8,128)S(1)}, f32[2,1,6,128]{3,2,1,0:T(8,128)S(1)}, u32[]{:S(2)}, u32[]{:S(2)}) collective-permute-start(f32[2,1,6,128]{3,2,1,0:T(8,128)S(1)} %get-tuple-element.1121), channel_id=1, source_target_pairs={{0,8},{8,16},{16,24},{24,0},{1,9},{9,17},{17,25},{25,1},{2,10},{10... | collective-permute-start | bytes 18440 | tf_op jit(solution)/shard_map/ppermute | solution.py:26
  340.8 3.7 collective-permute-start.29
  344.4 4.9 %collective-permute-start.30 = (f32[2,8,1,128]{3,2,1,0:T(1,128)S(1)}, f32[2,8,1,128]{3,2,1,0:T(1,128)S(1)}, u32[]{:S(2)}, u32[]{:S(2)}) collective-permute-start(f32[2,8,1,128]{3,2,1,0:T(1,128)S(1)} %get-tuple-element.1107), channel_id=1, source_target_pairs={{0,1},{1,2},{2,3},{3,4},{4,5},{5,6},{6,7},{7,0},{8,9},{9,10},{10,1... | collective-permute-start | bytes 24584 | tf_op jit(solution)/shard_map/ppermute | solution.py:26
  344.5 4.9 %collective-permute-start.31 = (f32[2,8,1,128]{3,2,1,0:T(1,128)S(1)}, f32[2,8,1,128]{3,2,1,0:T(1,128)S(1)}, u32[]{:S(2)}, u32[]{:S(2)}) collective-permute-start(f32[2,8,1,128]{3,2,1,0:T(1,128)S(1)} %get-tuple-element.1108), channel_id=1, source_target_pairs={{1,0},{2,1},{3,2},{4,3},{5,4},{6,5},{7,6},{0,7},{9,8},{10,9},{11,1... | collective-permute-start | bytes 24584 | tf_op jit(solution)/shard_map/ppermute | solution.py:29
  413.6 4.5 collective-permute-start.32
  419.5 4.9 %collective-permute-start.34 = (f32[8,1,128]{2,1,0:T(1,128)S(1)}, f32[8,1,128]{2,1,0:T(1,128)S(1)}, u32[]{:S(2)}, u32[]{:S(2)}) collective-permute-start(f32[8,1,128]{2,1,0:T(1,128)S(1)} %get-tuple-element.1137), channel_id=1, source_target_pairs={{0,1},{1,2},{2,3},{3,4},{4,5},{5,6},{6,7},{7,0},{8,9},{9,10},{10,1... | collective-permute-start | bytes 12296 | tf_op jit(solution)/shard_map/ppermute | solution.py:26
  419.6 4.9 %collective-permute-start.35 = (f32[8,1,128]{2,1,0:T(1,128)S(1)}, f32[8,1,128]{2,1,0:T(1,128)S(1)}, u32[]{:S(2)}, u32[]{:S(2)}) collective-permute-start(f32[8,1,128]{2,1,0:T(1,128)S(1)} %get-tuple-element.1138), channel_id=1, source_target_pairs={{1,0},{2,1},{3,2},{4,3},{5,4},{6,5},{7,6},{0,7},{9,8},{10,9},{11,1... | collective-permute-start | bytes 12296 | tf_op jit(solution)/shard_map/ppermute | solution.py:29
  (8 other events, 24.2 us)
where the time goes:
time: 454 us; the launch traced here: 453 us
  other arithmetic  169 us (37%)
  blocking collectives  154 us (34%)
  starting transfers between devices  60.1 us (13%)
  waiting for transfers between devices  31 us (7%)
  local copies, waits for them, and re-layouts  20.5 us (5%)
  loops' own time  17.7 us (4%)
    pmax x4, blocking collectives, global_bounds(): bounds = lax.pmax(jnp.concatenate([top_local, -low_local]), ('gx', 'gy'))  154 us
    reduce_sum x36, other arithmetic, pair_sums(): total_b = total_b + jnp.sum(pair_coef * diff_y, axis=-1)  89.8 us
    reduce_sum x24, other arithmetic, pair_sums(): jnp.sum(intersection * intersection * intersection, axis=-1)  48.3 us
    ppermute x18, starting transfers between devices, padded(): lax.ppermute(lax.slice_in_dim(block, 0, width, axis=dim), axis, backward)  39 us
    ppermute x18, starting transfers between devices, padded(): lax.ppermute(lax.slice_in_dim(block, block.shape[dim] - width, None, axis...  21.1 us
    ppermute x18, waiting for transfers between devices, padded(): lax.ppermute(lax.slice_in_dim(block, block.shape[dim] - width, None, axis...  20.8 us
    another operation x8, loops' own time, blocked(): results = lax.map(one_block, jnp.arange(block_count, dtype=jnp.int32))  17.7 us
    dynamic_slice x24, local copies, waits for them, and re-layouts, blocked(): results = lax.map(one_block, jnp.arange(block_count, dtype=jnp.int32))  14.1 us
  transfers between devices with their start and end apart: 36, of which 22 were waited for; matrix products, arithmetic and copies ran while one was open for 0% of the time, Pallas kernels for 0%

commit v1 on v0

--- a/solution.py
+++ b/solution.py
@@ -1,6 +1,8 @@
 import jax
 import jax.numpy as jnp
 from jax import lax
+from jax.experimental import pallas as pl
+from jax.experimental.pallas import tpu as pltpu
 from jax.sharding import PartitionSpec as P
 
 ITERS = 4
@@ -31,57 +33,238 @@
     return block
 
 
-def window_of(source, off_x, off_y, row_count, col_count):
-    return source[1 + off_x : 1 + off_x + row_count, 1 + off_y : 1 + off_y + col_count]
-
-
-def pair_sums(centers, padded_list, with_force):
-    center_x, center_y = (centers[0], centers[1])
-    near_x, near_y, near_live = (padded_list[0], padded_list[1], padded_list[2])
-    row_count, col_count = (center_x.shape[0], center_x.shape[1])
-    total_a = jnp.zeros_like(center_x)
-    total_b = jnp.zeros_like(center_x)
-    for off_x in (-1, 0, 1):
-        for off_y in (-1, 0, 1):
-            other_x = window_of(near_x, off_x, off_y, row_count, col_count)
-            other_y = window_of(near_y, off_x, off_y, row_count, col_count)
-            other_live = window_of(near_live, off_x, off_y, row_count, col_count)
-            diff_x = center_x[..., :, None] - (other_x[..., None, :] + off_x)
-            diff_y = center_y[..., :, None] - (other_y[..., None, :] + off_y)
-            intersection = (
-                jnp.maximum(1.0 - diff_x * diff_x - diff_y * diff_y, 0.0) * other_live[..., None, :]
-            )
-            if with_force:
-                other_term = window_of(padded_list[3], off_x, off_y, row_count, col_count)
-                pair_coef = (
-                    intersection
-                    * intersection
-                    * (centers[2][..., :, None] + other_term[..., None, :])
+EMPTY = -1e30
+
+
+def split3(value):
+    high = value.astype(jnp.bfloat16).astype(jnp.float32)
+    rest = value - high
+    mid = rest.astype(jnp.bfloat16).astype(jnp.float32)
+    low = (rest - mid).astype(jnp.bfloat16).astype(jnp.float32)
+    return high, mid, low
+
+
+def put_rows(ref, row, values, width):
+    for at, value in enumerate(values):
+        ref[row, at * width : (at + 1) * width, :] = value
+
+
+def source_features(x, y, live, jf, row, width):
+    x = jnp.where(live, x - 0.5, 0.0)
+    y = jnp.where(live, y - 0.5, 0.0)
+    xh, xm, xl = split3(x)
+    yh, ym, yl = split3(y)
+    bh, bm, bl = split3(jnp.where(live, -(x * x + y * y), EMPTY))
+    one = jnp.ones_like(x)
+    nil = jnp.zeros_like(x)
+    put_rows(
+        jf,
+        row,
+        [xh, xh, xm, xh, xl, xm, bh, bm, yh, yh, ym, yh, yl, ym, bl, nil]
+        + [one, one, one, nil, nil, nil, nil, nil],
+        width,
+    )
+
+
+def pair_features(jf, lhs, row, width, half):
+    for n in range(width - half):
+        first = jf[row, pl.ds(n, 24, stride=width), :]
+        second = jf[row, pl.ds(n + half, 24, stride=width), :]
+        both = jnp.concatenate([first, second], axis=0)
+        lhs[row, n] = both.T.astype(jnp.bfloat16)
+
+
+def target_features(x, y, xf, yf, af, row, width):
+    x = x - 0.5
+    y = y - 0.5
+    one = jnp.ones_like(x)
+    nil = jnp.zeros_like(x)
+    for at in range(3):
+        h, m, l = split3(2.0 * (x - (at - 1.0)))
+        put_rows(xf.at[row], at, [h, m, h, l, h, m, one, one], width)
+        h, m, l = split3(2.0 * (y - (at - 1.0)))
+        put_rows(yf.at[row], at, [h, m, h, l, h, m, one, nil], width)
+    for ax in range(3):
+        for ay in range(3):
+            dx = x - (ax - 1.0)
+            dy = y - (ay - 1.0)
+            h, m, l = split3(1.0 - (dx * dx + dy * dy))
+            put_rows(af.at[row], 3 * ax + ay, [h, m, l, nil, nil, nil, nil, nil], width)
+
+
+def target_block(xf, yf, af, row, cell, ax, ay, width):
+    return jnp.concatenate(
+        [
+            xf[row, ax, pl.ds(cell + 1, 8, stride=width), :],
+            yf[row, ay, pl.ds(cell + 1, 8, stride=width), :],
+            af[row, 3 * ax + ay, pl.ds(cell + 1, 8, stride=width), :],
+        ],
+        axis=0,
+    )
+
+
+def overlap(lhs, xf, yf, af, row, cell, ax, ay, width, half):
+    first = target_block(xf, yf, af, row, cell, ax, ay, width)
+    second = target_block(xf, yf, af, row, cell + half, ax, ay, width)
+    nil = jnp.zeros_like(first)
+    rhs = jnp.concatenate(
+        [
+            jnp.concatenate([first, nil], axis=1),
+            jnp.concatenate([nil, second], axis=1),
+        ],
+        axis=0,
+    ).astype(jnp.bfloat16)
+    raw = jnp.dot(lhs[row + ax, cell + ay], rhs, preferred_element_type=jnp.float32)
+    return jnp.maximum(raw, 0.0)
+
+
+def all_features(pos, live, jf, lhs, xf, yf, af, rows, width, half):
+    def source_row(row, carry):
+        source_features(pos[0, row], pos[1, row], live[row] > 0, jf, row, width)
+        pair_features(jf, lhs, row, width, half)
+        return carry
+
+    lax.fori_loop(0, rows + 2, source_row, 0)
+
+    def target_row(row, carry):
+        target_features(pos[0, row + 1], pos[1, row + 1], xf, yf, af, row, width)
+        return carry
+
+    lax.fori_loop(0, rows, target_row, 0)
+
+
+def density_kernel(pos, live, out, jf, lhs, xf, yf, af):
+    rows, cols, slots = out.shape
+    width, half = cols + 2, cols // 2
+    all_features(pos, live, jf, lhs, xf, yf, af, rows, width, half)
+
+    def one_row(row, carry):
+        for cell in range(half):
+            total = jnp.zeros((8, 2 * slots), jnp.float32)
+            for ax in range(3):
+                for ay in range(3):
+                    w = overlap(lhs, xf, yf, af, row, cell, ax, ay, width, half)
+                    cube = w * w * w
+                    total = total + jnp.sum(cube.reshape(slots // 8, 8, 2 * slots), axis=0)
+            dens = jnp.sum(total, axis=0, keepdims=True)
+            out[row, cell : cell + 1, :] = dens[:, :slots]
+            out[row, cell + half : cell + half + 1, :] = dens[:, slots:]
+        return carry
+
+    lax.fori_loop(0, rows, one_row, 0)
+
+
+def value_rows(x, y, term, live, vf, row, width):
+    x = jnp.where(live, x - 0.5, 0.0)
+    y = jnp.where(live, y - 0.5, 0.0)
+    term = jnp.where(live, term, 0.0)
+    highs, mids = [], []
+    for value in (jnp.ones_like(x), x, y, term, term * x, term * y):
+        high, mid, _ = split3(value)
+        highs.append(high)
+        mids.append(mid)
+    nil = jnp.zeros_like(x)
+    put_rows(vf, row, highs + [nil, nil] + mids + [nil, nil], width)
+
+
+def force_kernel(pos, live, term, out, jf, lhs, xf, yf, af, vf, sums):
+    _, rows, cols, slots = out.shape
+    width, half = cols + 2, cols // 2
+    all_features(pos, live, jf, lhs, xf, yf, af, rows, width, half)
+
+    def value_row(row, carry):
+        value_rows(pos[0, row], pos[1, row], term[row], live[row] > 0, vf, row, width)
+        return carry
+
+    lax.fori_loop(0, rows + 2, value_row, 0)
+
+    def one_row(row, carry):
+        for cell in range(half):
+            zero = jnp.zeros((8, slots), jnp.float32)
+            parts = [[zero, zero, zero], [zero, zero, zero]]
+            for ax in range(3):
+                for ay in range(3):
+                    w = overlap(lhs, xf, yf, af, row, cell, ax, ay, width, half)
+                    square = w * w
+                    high = square.astype(jnp.bfloat16)
+                    low = (square - high.astype(jnp.float32)).astype(jnp.bfloat16)
+                    value = jnp.concatenate(
+                        [
+                            vf[row + ax, pl.ds(cell + ay, 16, stride=width), :],
+                            vf[row + ax, pl.ds(cell + ay + half, 16, stride=width), :],
+                        ],
+                        axis=0,
+                    ).astype(jnp.bfloat16)
+                    got = jnp.dot(value, high, preferred_element_type=jnp.float32) + jnp.dot(
+                        value, low, preferred_element_type=jnp.float32
+                    )
+                    pieces = (
+                        got[0:8, :slots] + got[8:16, :slots],
+                        got[16:24, slots:] + got[24:32, slots:],
+                    )
+                    for acc, piece in zip(parts, pieces):
+                        acc[0] = acc[0] + piece
+                        if ax != 1:
+                            acc[1] = acc[1] + piece if ax == 2 else acc[1] - piece
+                        if ay != 1:
+                            acc[2] = acc[2] + piece if ay == 2 else acc[2] - piece
+            for at, acc in zip((cell, cell + half), parts):
+                plain, by_x, by_y = acc
+                rows_out = (
+                    plain[0:1],
+                    plain[1:2] + by_x[0:1],
+                    plain[2:3] + by_y[0:1],
+                    plain[3:4],
+                    plain[4:5] + by_x[3:4],
+                    plain[5:6] + by_y[3:4],
                 )
-                total_a = total_a + jnp.sum(pair_coef * diff_x, axis=-1)
-                total_b = total_b + jnp.sum(pair_coef * diff_y, axis=-1)
-            else:
-                total_a = total_a + jnp.sum(intersection * intersection * intersection, axis=-1)
-    if with_force:
-        return (total_a, total_b)
-    return (total_a,)
-
-
-def blocked(with_force, centers, padded_list, row_count):
-    block_count = row_count // 2
-
-    def one_block(block_index):
-        first_row = block_index * 2
-        center_part = tuple(
-            (lax.dynamic_slice_in_dim(source, first_row, 2, 0) for source in centers)
-        )
-        padded_part = tuple(
-            (lax.dynamic_slice_in_dim(source, first_row, 4, 0) for source in padded_list)
-        )
-        return pair_sums(center_part, padded_part, with_force)
-
-    results = lax.map(one_block, jnp.arange(block_count, dtype=jnp.int32))
-    return tuple((source.reshape((row_count,) + source.shape[2:]) for source in results))
+                for k, value in enumerate(rows_out):
+                    sums[k, at + 1 : at + 2, :] = value
+        own_x = pos[0, row + 1] - 0.5
+        own_y = pos[1, row + 1] - 0.5
+        own_term = term[row + 1]
+        force_x = own_term * (own_x * sums[0] - sums[1]) + own_x * sums[3] - sums[4]
+        force_y = own_term * (own_y * sums[0] - sums[2]) + own_y * sums[3] - sums[5]
+        out[0, row] = force_x[1 : cols + 1]
+        out[1, row] = force_y[1 : cols + 1]
+        return carry
+
+    lax.fori_loop(0, rows, one_row, 0)
+
+
+def feature_scratch(rows, cols, slots):
+    width, half = cols + 2, cols // 2
+    return [
+        pltpu.VMEM((rows + 2, 24 * width, slots), jnp.float32),
+        pltpu.VMEM((rows + 2, width - half, slots, 48), jnp.bfloat16),
+        pltpu.VMEM((rows, 3, 8 * width, slots), jnp.float32),
+        pltpu.VMEM((rows, 3, 8 * width, slots), jnp.float32),
+        pltpu.VMEM((rows, 9, 8 * width, slots), jnp.float32),
+    ]
+
+
+def density_sums(moved, cycle_mask):
+    _, rows, cols, slots = moved.shape
+    rows, cols = rows - 2, cols - 2
+    return pl.pallas_call(
+        density_kernel,
+        out_shape=jax.ShapeDtypeStruct((rows, cols, slots), jnp.float32),
+        scratch_shapes=feature_scratch(rows, cols, slots),
+    )(moved, cycle_mask)
+
+
+def force_sums(moved, cycle_mask, near_term):
+    _, rows, cols, slots = moved.shape
+    rows, cols = rows - 2, cols - 2
+    return pl.pallas_call(
+        force_kernel,
+        out_shape=jax.ShapeDtypeStruct((2, rows, cols, slots), jnp.float32),
+        scratch_shapes=feature_scratch(rows, cols, slots)
+        + [
+            pltpu.VMEM((rows + 2, 16 * (cols + 2), slots), jnp.float32),
+            pltpu.VMEM((6, cols + 2, slots), jnp.float32),
+        ],
+    )(moved, cycle_mask, near_term)
 
 
 def global_bounds(density_ratio, live_bool, heavy_bool):
@@ -147,14 +330,12 @@
         pos_x = position[0] + TIME_STEP * vel_x
         pos_y = position[1] + TIME_STEP * vel_y
         moved = padded(jnp.stack([pos_x, pos_y]), (("gx", 1), ("gy", 2)), 1)
-        (density_sum,) = blocked(False, (pos_x, pos_y), (moved[0], moved[1], cycle_mask), tile_rows)
+        density_sum = density_sums(moved, cycle_mask)
         pressure, press_term, monitor_row = pressure_update(
             pressure, density_sum, live_bool, heavy_bool, live_bool, heavy_bool
         )
         near_term = padded(press_term, (("gx", 0), ("gy", 1)), 1)
-        force_x, force_y = blocked(
-            True, (pos_x, pos_y, press_term), (moved[0], moved[1], cycle_mask, near_term), tile_rows
-        )
+        force_x, force_y = force_sums(moved, cycle_mask, near_term)
         accel_x = live_mask * (6.0 * KERNEL_NORM / particle_mass) * force_x
         accel_y = live_mask * (6.0 * KERNEL_NORM / particle_mass) * force_y
         monitor_rows.append(monitor_row)

time: 454 us -> 361 us (0.80)
  other arithmetic: 169 us -> 41.1 us
  Pallas kernels: 0 us -> 68 us
  loops' own time: 17.7 us -> 0 us
  local copies, waits for them, and re-layouts: 20.5 us -> 5.5 us
    reduce_sum x60 -> x0, other arithmetic: 138 us -> none  [the longest x36 89.8 us: pair_sums(): total_b = total_b + jnp.sum(pair_coef * diff_y, axis=-1)]
    pallas_call x0 -> x8, Pallas kernels: none -> 68 us  [the longest x4 41.1 us: force_sums(): pl.pallas_call(force_kernel, out_shape=jax.ShapeDtypeStruct((2, rows, col...]
    another operation x8 -> x0, loops' own time: 17.7 us -> none  [blocked(): results = lax.map(one_block, jnp.arange(block_count, dtype=jnp.int32))]
    dynamic_slice x48 -> x0, local copies, waits for them, and re-layouts: 14.4 us -> none  [the longest x24 14.1 us: blocked(): results = lax.map(one_block, jnp.arange(block_count, dtype=jnp.int32))]
    concatenate x8, other arithmetic: 0.17 us -> 5.09 us  [padded(): block = jnp.concatenate([low, block, high], axis=dim)]
where the time goes in v1:
time: 361 us; the launch traced here: 360 us
  blocking collectives  154 us (43%)
  Pallas kernels  68 us (19%)
  starting transfers between devices  60.1 us (17%)
  other arithmetic  41.1 us (11%)
  waiting for transfers between devices  30.4 us (8%)
  local copies, waits for them, and re-layouts  5.5 us (2%)
    pmax x4, blocking collectives, global_bounds(): bounds = lax.pmax(jnp.concatenate([top_local, -low_local]), ('gx', 'gy'))  154 us
    pallas_call x4, Pallas kernels, force_sums(): pl.pallas_call(force_kernel, out_shape=jax.ShapeDtypeStruct((2, rows, col...  41.1 us
    ppermute x18, starting transfers between devices, padded(): lax.ppermute(lax.slice_in_dim(block, 0, width, axis=dim), axis, backward)  39 us
    pallas_call x4, Pallas kernels, density_sums(): pl.pallas_call(density_kernel, out_shape=jax.ShapeDtypeStruct((rows, cols...  26.9 us
    ppermute x18, starting transfers between devices, padded(): lax.ppermute(lax.slice_in_dim(block, block.shape[dim] - width, None, axis...  21.1 us
    ppermute x18, waiting for transfers between devices, padded(): lax.ppermute(lax.slice_in_dim(block, block.shape[dim] - width, None, axis...  20.2 us
    select_n x4, other arithmetic, pressure_update(): jnp.where(live_bool, pressure / (safe_density * safe_density), 0.0)  13.5 us
    ppermute x18, waiting for transfers between devices, padded(): lax.ppermute(lax.slice_in_dim(block, 0, width, axis=dim), axis, backward)  10.2 us
  transfers between devices with their start and end apart: 36, of which 22 were waited for; matrix products, arithmetic and copies ran while one was open for 0% of the time, Pallas kernels for 0%

profile of v1, /device:TPU:0, one launch (start us, length us, event | category | flops | bytes accessed | tf_op | source)
XLA Modules:
  0.0 359.6 jit_solution(11277981982632242433)
XLA Ops:
  2.4 3.0 collective-permute-start
  9.6 3.5 collective-permute-start.3
  13.2 3.5 collective-permute-start.7
  18.7 6.7 %shard_map.84 = f32[6,6,128]{2,1,0:T(8,128)} custom-call(f32[2,8,8,128]{3,2,1,0:T(8,128)} %pad_maximum_fusion.pos, f32[8,8,128]{2,1,0:T(8,128)} %fusion.1.live), custom_call_target="tpu_custom_call" | custom-call | tf_op jit(solution)/shard_map/pallas_call | solution.py:249
  29.8 39.1 %pmax.28 = f32[4]{0:T(128)S(1)} all-reduce(f32[4]{0:T(128)S(1)} %pad_maximum_fusion.47), channel_id=1, replica_groups=mesh['gx'=4,'gy'=8] {'gx','gy'}, use_global_device_ids=true, to_apply=%region_4.5 | all-reduce | flops 4 | bytes 32 | tf_op jit(solution)/shard_map/pmax | solution.py:285
  70.9 2.3 collective-permute-start.8
  76.9 3.5 collective-permute-start.11
  82.4 10.3 %shard_map.85 = f32[2,6,6,128]{3,2,1,0:T(8,128)} custom-call(f32[2,8,8,128]{3,2,1,0:T(8,128)} %pad_maximum_fusion.pos, f32[8,8,128]{2,1,0:T(8,128)} %fusion.1.live, f32[8,8,128]{2,1,0:T(8,128)} %pad_maximum_fusion.6.term), custom_call_target="tpu_custom_call" | custom-call | tf_op jit(solution)/shard_map/pallas_call | solution.py:259
  93.6 2.4 collective-permute-start.12
  99.7 3.5 collective-permute-start.15
  105.3 6.7 %shard_map.86 = f32[6,6,128]{2,1,0:T(8,128)} custom-call(f32[2,8,8,128]{3,2,1,0:T(8,128)} %pad_maximum_fusion.1.pos, f32[8,8,128]{2,1,0:T(8,128)} %fusion.1.live), custom_call_target="tpu_custom_call" | custom-call | tf_op jit(solution)/shard_map/pallas_call | solution.py:249
  116.2 38.1 %pmax.29 = f32[4]{0:T(128)S(1)} all-reduce(f32[4]{0:T(128)S(1)} %pad_maximum_fusion.48), channel_id=1, replica_groups=mesh['gx'=4,'gy'=8] {'gx','gy'}, use_global_device_ids=true, to_apply=%region_9.10 | all-reduce | flops 4 | bytes 32 | tf_op jit(solution)/shard_map/pmax | solution.py:285
  155.1 2.6 divide_select_fusion.2
  157.7 2.3 collective-permute-start.16
  163.7 3.5 collective-permute-start.19
  169.2 10.3 %shard_map.87 = f32[2,6,6,128]{3,2,1,0:T(8,128)} custom-call(f32[2,8,8,128]{3,2,1,0:T(8,128)} %pad_maximum_fusion.1.pos, f32[8,8,128]{2,1,0:T(8,128)} %fusion.1.live, f32[8,8,128]{2,1,0:T(8,128)} %pad_maximum_fusion.7.term), custom_call_target="tpu_custom_call" | custom-call | tf_op jit(solution)/shard_map/pallas_call | solution.py:259
  180.3 2.4 collective-permute-start.20
  186.5 3.5 collective-permute-start.23
  192.0 6.7 %shard_map.88 = f32[6,6,128]{2,1,0:T(8,128)} custom-call(f32[2,8,8,128]{3,2,1,0:T(8,128)} %pad_maximum_fusion.2.pos, f32[8,8,128]{2,1,0:T(8,128)} %fusion.1.live), custom_call_target="tpu_custom_call" | custom-call | tf_op jit(solution)/shard_map/pallas_call | solution.py:249
  203.0 38.2 %pmax.30 = f32[4]{0:T(128)S(1)} all-reduce(f32[4]{0:T(128)S(1)} %pad_maximum_fusion.49), channel_id=1, replica_groups=mesh['gx'=4,'gy'=8] {'gx','gy'}, use_global_device_ids=true, to_apply=%region_14.15 | all-reduce | flops 4 | bytes 32 | tf_op jit(solution)/shard_map/pmax | solution.py:285
  241.9 3.8 %divide_select_fusion.1 = f32[6,6,128]{2,1,0:T(8,128)S(1)} fusion(f32[6,6,128]{2,1,0:T(8,128)S(1)} %copy-done.3, s32[6,6]{1,0:T(8,128)S(1)} %copy-done.2, pred[6,6,128]{2,1,0:T(8,128)(4,1)S(1)} %get-tuple-element.40, f32[]{:T(128)} %bitcast.31, f32[]{:T(128)} %bitcast.30, f32[]{:T(128)} %bitcast.21, f32[]{:T(128)} %bitcast.20, f32[]{:T(128)} %bitcast.8, ...), kind=kLoop, calls=%fused_computation.120 | loop fusion | flops 138240 | bytes 78504 | tf_op jit(solution)/shard_map/jit(_where)/select_n | solution.py:307
  245.8 2.3 collective-permute-start.24
  251.8 3.5 collective-permute-start.27
  257.3 10.3 %shard_map.89 = f32[2,6,6,128]{3,2,1,0:T(8,128)} custom-call(f32[2,8,8,128]{3,2,1,0:T(8,128)} %pad_maximum_fusion.2.pos, f32[8,8,128]{2,1,0:T(8,128)} %fusion.1.live, f32[8,8,128]{2,1,0:T(8,128)} %pad_maximum_fusion.8.term), custom_call_target="tpu_custom_call" | custom-call | tf_op jit(solution)/shard_map/pallas_call | solution.py:259
  268.4 2.4 collective-permute-start.28
  274.5 3.5 collective-permute-start.31
  280.1 6.7 %shard_map.90 = f32[6,6,128]{2,1,0:T(8,128)} custom-call(f32[2,8,8,128]{3,2,1,0:T(8,128)} %pad_maximum_fusion.3.pos, f32[8,8,128]{2,1,0:T(8,128)} %fusion.1.live), custom_call_target="tpu_custom_call" | custom-call | tf_op jit(solution)/shard_map/pallas_call | solution.py:249
  291.1 38.1 %pmax.31 = f32[4]{0:T(128)S(1)} all-reduce(f32[4]{0:T(128)S(1)} %pad_maximum_fusion.50), channel_id=1, replica_groups=mesh['gx'=4,'gy'=8] {'gx','gy'}, use_global_device_ids=true, to_apply=%region_19.20 | all-reduce | flops 4 | bytes 32 | tf_op jit(solution)/shard_map/pmax | solution.py:285
  329.9 5.8 %divide_select_fusion = (f32[6,6,128]{2,1,0:T(8,128)S(1)}, f32[6,6,128]{2,1,0:T(8,128)}) fusion(f32[6,6,128]{2,1,0:T(8,128)S(1)} %copy-done.4, s32[6,6]{1,0:T(8,128)S(1)} %copy-done.2, pred[6,6,128]{2,1,0:T(8,128)(4,1)S(1)} %get-tuple-element.40, f32[]{:T(128)} %bitcast.41, f32[]{:T(128)} %bitcast.40, f32[6,6,128]{2,1,0:T(8,128)S(1)} %copy-done.3, ...), kind=kLoop, calls=%fused_computation.115 | loop fusion | flops 175104 | bytes 115376 | tf_op jit(solution)/shard_map/jit(_where)/select_n | solution.py:307
  335.7 2.3 collective-permute-start.32
  341.7 3.5 collective-permute-start.35
  347.1 10.3 %shard_map.91 = f32[2,6,6,128]{3,2,1,0:T(8,128)} custom-call(f32[2,8,8,128]{3,2,1,0:T(8,128)} %pad_maximum_fusion.3.pos, f32[8,8,128]{2,1,0:T(8,128)} %fusion.1.live, f32[8,8,128]{2,1,0:T(8,128)} %pad_maximum_fusion.9.term), custom_call_target="tpu_custom_call" | custom-call | tf_op jit(solution)/shard_map/pallas_call | solution.py:259
  (137 shorter events, 73.6 us)
Async XLA Ops:
  2.4 7.1 %collective-permute-start = (f32[2,1,6,128]{3,2,1,0:T(8,128)S(1)}, f32[2,1,6,128]{3,2,1,0:T(8,128)S(1)}, u32[]{:S(2)}, u32[]{:S(2)}) collective-permute-start(f32[2,1,6,128]{3,2,1,0:T(8,128)S(1)} %get-tuple-element.63), channel_id=1, source_target_pairs={{0,8},{8,16},{16,24},{24,0},{1,9},{9,17},{17,25},{25,1},{2,10},{10... | collective-permute-start | bytes 18440 | tf_op jit(solution)/shard_map/ppermute | solution.py:28
  5.4 4.1 %collective-permute-start.1 = (f32[2,1,6,128]{3,2,1,0:T(8,128)S(1)}, f32[2,1,6,128]{3,2,1,0:T(8,128)S(1)}, u32[]{:S(2)}, u32[]{:S(2)}) collective-permute-start(f32[2,1,6,128]{3,2,1,0:T(8,128)S(1)} %get-tuple-element.64), channel_id=1, source_target_pairs={{8,0},{16,8},{24,16},{0,24},{9,1},{17,9},{25,17},{1,25},{10,2},{18... | collective-permute-start | bytes 18440 | tf_op jit(solution)/shard_map/ppermute | solution.py:31
  6.5 6.6 %collective-permute-start.4 = (s32[2,6,128]{2,1,0:T(8,128)S(1)}, s32[2,6,128]{2,1,0:T(8,128)S(1)}, u32[]{:S(2)}, u32[]{:S(2)}) collective-permute-start(s32[2,6,128]{2,1,0:T(8,128)S(1)} %get-tuple-element.89), channel_id=1, source_target_pairs={{0,8},{8,16},{16,24},{24,0},{1,9},{9,17},{17,25},{25,1},{2,10},{10... | collective-permute-start | bytes 18440 | tf_op jit(solution)/shard_map/ppermute | solution.py:28
  7.6 5.5 %collective-permute-start.5 = (s32[2,6,128]{2,1,0:T(8,128)S(1)}, s32[2,6,128]{2,1,0:T(8,128)S(1)}, u32[]{:S(2)}, u32[]{:S(2)}) collective-permute-start(s32[2,6,128]{2,1,0:T(8,128)S(1)} %get-tuple-element.90), channel_id=1, source_target_pairs={{8,0},{16,8},{24,16},{0,24},{9,1},{17,9},{25,17},{1,25},{10,2},{18... | collective-permute-start | bytes 18440 | tf_op jit(solution)/shard_map/ppermute | solution.py:31
  9.5 7.2 %collective-permute-start.2 = (f32[2,8,1,128]{3,2,1,0:T(1,128)S(1)}, f32[2,8,1,128]{3,2,1,0:T(1,128)S(1)}, u32[]{:S(2)}, u32[]{:S(2)}) collective-permute-start(f32[2,8,1,128]{3,2,1,0:T(1,128)S(1)} %get-tuple-element.47), channel_id=1, source_target_pairs={{0,1},{1,2},{2,3},{3,4},{4,5},{5,6},{6,7},{7,0},{8,9},{9,10},{10,1... | collective-permute-start | bytes 24584 | tf_op jit(solution)/shard_map/ppermute | solution.py:28
  9.6 7.2 %collective-permute-start.3 = (f32[2,8,1,128]{3,2,1,0:T(1,128)S(1)}, f32[2,8,1,128]{3,2,1,0:T(1,128)S(1)}, u32[]{:S(2)}, u32[]{:S(2)}) collective-permute-start(f32[2,8,1,128]{3,2,1,0:T(1,128)S(1)} %get-tuple-element.48), channel_id=1, source_target_pairs={{1,0},{2,1},{3,2},{4,3},{5,4},{6,5},{7,6},{0,7},{9,8},{10,9},{11,1... | collective-permute-start | bytes 24584 | tf_op jit(solution)/shard_map/ppermute | solution.py:31
  13.1 4.9 %collective-permute-start.6 = (s32[10,2,128]{2,1,0:T(2,128)S(1)}, s32[10,2,128]{2,1,0:T(2,128)S(1)}, u32[]{:S(2)}, u32[]{:S(2)}) collective-permute-start(s32[10,2,128]{2,1,0:T(2,128)S(1)} %get-tuple-element.65), channel_id=1, source_target_pairs={{0,1},{1,2},{2,3},{3,4},{4,5},{5,6},{6,7},{7,0},{8,9},{9,10},{10,1... | collective-permute-start | bytes 30728 | tf_op jit(solution)/shard_map/ppermute | solution.py:28
  13.2 4.9 %collective-permute-start.7 = (s32[10,2,128]{2,1,0:T(2,128)S(1)}, s32[10,2,128]{2,1,0:T(2,128)S(1)}, u32[]{:S(2)}, u32[]{:S(2)}) collective-permute-start(s32[10,2,128]{2,1,0:T(2,128)S(1)} %get-tuple-element.66), channel_id=1, source_target_pairs={{1,0},{2,1},{3,2},{4,3},{5,4},{6,5},{7,6},{0,7},{9,8},{10,9},{11,1... | collective-permute-start | bytes 30728 | tf_op jit(solution)/shard_map/ppermute | solution.py:31
  70.9 4.6 %collective-permute-start.8 = (f32[1,6,128]{2,1,0:T(8,128)S(1)}, f32[1,6,128]{2,1,0:T(8,128)S(1)}, u32[]{:S(2)}, u32[]{:S(2)}) collective-permute-start(f32[1,6,128]{2,1,0:T(8,128)S(1)} %get-tuple-element.87), channel_id=1, source_target_pairs={{0,8},{8,16},{16,24},{24,0},{1,9},{9,17},{17,25},{25,1},{2,10},{10... | collective-permute-start | bytes 9224 | tf_op jit(solution)/shard_map/ppermute | solution.py:28
  76.9 4.9 %collective-permute-start.10 = (f32[8,1,128]{2,1,0:T(1,128)S(1)}, f32[8,1,128]{2,1,0:T(1,128)S(1)}, u32[]{:S(2)}, u32[]{:S(2)}) collective-permute-start(f32[8,1,128]{2,1,0:T(1,128)S(1)} %get-tuple-element.79), channel_id=1, source_target_pairs={{0,1},{1,2},{2,3},{3,4},{4,5},{5,6},{6,7},{7,0},{8,9},{9,10},{10,1... | collective-permute-start | bytes 12296 | tf_op jit(solution)/shard_map/ppermute | solution.py:28
  76.9 4.9 %collective-permute-start.11 = (f32[8,1,128]{2,1,0:T(1,128)S(1)}, f32[8,1,128]{2,1,0:T(1,128)S(1)}, u32[]{:S(2)}, u32[]{:S(2)}) collective-permute-start(f32[8,1,128]{2,1,0:T(1,128)S(1)} %get-tuple-element.80), channel_id=1, source_target_pairs={{1,0},{2,1},{3,2},{4,3},{5,4},{6,5},{7,6},{0,7},{9,8},{10,9},{11,1... | collective-permute-start | bytes 12296 | tf_op jit(solution)/shard_map/ppermute | solution.py:31
  93.6 4.6 %collective-permute-start.12 = (f32[2,1,6,128]{3,2,1,0:T(8,128)S(1)}, f32[2,1,6,128]{3,2,1,0:T(8,128)S(1)}, u32[]{:S(2)}, u32[]{:S(2)}) collective-permute-start(f32[2,1,6,128]{3,2,1,0:T(8,128)S(1)} %get-tuple-element.61), channel_id=1, source_target_pairs={{0,8},{8,16},{16,24},{24,0},{1,9},{9,17},{17,25},{25,1},{2,10},{10... | collective-permute-start | bytes 18440 | tf_op jit(solution)/shard_map/ppermute | solution.py:28
  96.0 3.7 %collective-permute-start.13 = (f32[2,1,6,128]{3,2,1,0:T(8,128)S(1)}, f32[2,1,6,128]{3,2,1,0:T(8,128)S(1)}, u32[]{:S(2)}, u32[]{:S(2)}) collective-permute-start(f32[2,1,6,128]{3,2,1,0:T(8,128)S(1)} %get-tuple-element.62), channel_id=1, source_target_pairs={{8,0},{16,8},{24,16},{0,24},{9,1},{17,9},{25,17},{1,25},{10,2},{18... | collective-permute-start | bytes 18440 | tf_op jit(solution)/shard_map/ppermute | solution.py:31
  99.6 4.9 %collective-permute-start.14 = (f32[2,8,1,128]{3,2,1,0:T(1,128)S(1)}, f32[2,8,1,128]{3,2,1,0:T(1,128)S(1)}, u32[]{:S(2)}, u32[]{:S(2)}) collective-permute-start(f32[2,8,1,128]{3,2,1,0:T(1,128)S(1)} %get-tuple-element.45), channel_id=1, source_target_pairs={{0,1},{1,2},{2,3},{3,4},{4,5},{5,6},{6,7},{7,0},{8,9},{9,10},{10,1... | collective-permute-start | bytes 24584 | tf_op jit(solution)/shard_map/ppermute | solution.py:28
  99.7 4.9 %collective-permute-start.15 = (f32[2,8,1,128]{3,2,1,0:T(1,128)S(1)}, f32[2,8,1,128]{3,2,1,0:T(1,128)S(1)}, u32[]{:S(2)}, u32[]{:S(2)}) collective-permute-start(f32[2,8,1,128]{3,2,1,0:T(1,128)S(1)} %get-tuple-element.46), channel_id=1, source_target_pairs={{1,0},{2,1},{3,2},{4,3},{5,4},{6,5},{7,6},{0,7},{9,8},{10,9},{11,1... | collective-permute-start | bytes 24584 | tf_op jit(solution)/shard_map/ppermute | solution.py:31
  157.7 4.6 %collective-permute-start.16 = (f32[1,6,128]{2,1,0:T(8,128)S(1)}, f32[1,6,128]{2,1,0:T(8,128)S(1)}, u32[]{:S(2)}, u32[]{:S(2)}) collective-permute-start(f32[1,6,128]{2,1,0:T(8,128)S(1)} %get-tuple-element.85), channel_id=1, source_target_pairs={{0,8},{8,16},{16,24},{24,0},{1,9},{9,17},{17,25},{25,1},{2,10},{10... | collective-permute-start | bytes 9224 | tf_op jit(solution)/shard_map/ppermute | solution.py:28
  163.6 4.9 %collective-permute-start.18 = (f32[8,1,128]{2,1,0:T(1,128)S(1)}, f32[8,1,128]{2,1,0:T(1,128)S(1)}, u32[]{:S(2)}, u32[]{:S(2)}) collective-permute-start(f32[8,1,128]{2,1,0:T(1,128)S(1)} %get-tuple-element.77), channel_id=1, source_target_pairs={{0,1},{1,2},{2,3},{3,4},{4,5},{5,6},{6,7},{7,0},{8,9},{9,10},{10,1... | collective-permute-start | bytes 12296 | tf_op jit(solution)/shard_map/ppermute | solution.py:28
  163.7 4.9 %collective-permute-start.19 = (f32[8,1,128]{2,1,0:T(1,128)S(1)}, f32[8,1,128]{2,1,0:T(1,128)S(1)}, u32[]{:S(2)}, u32[]{:S(2)}) collective-permute-start(f32[8,1,128]{2,1,0:T(1,128)S(1)} %get-tuple-element.78), channel_id=1, source_target_pairs={{1,0},{2,1},{3,2},{4,3},{5,4},{6,5},{7,6},{0,7},{9,8},{10,9},{11,1... | collective-permute-start | bytes 12296 | tf_op jit(solution)/shard_map/ppermute | solution.py:31
  180.3 4.6 %collective-permute-start.20 = (f32[2,1,6,128]{3,2,1,0:T(8,128)S(1)}, f32[2,1,6,128]{3,2,1,0:T(8,128)S(1)}, u32[]{:S(2)}, u32[]{:S(2)}) collective-permute-start(f32[2,1,6,128]{3,2,1,0:T(8,128)S(1)} %get-tuple-element.59), channel_id=1, source_target_pairs={{0,8},{8,16},{16,24},{24,0},{1,9},{9,17},{17,25},{25,1},{2,10},{10... | collective-permute-start | bytes 18440 | tf_op jit(solution)/shard_map/ppermute | solution.py:28
  182.7 3.7 %collective-permute-start.21 = (f32[2,1,6,128]{3,2,1,0:T(8,128)S(1)}, f32[2,1,6,128]{3,2,1,0:T(8,128)S(1)}, u32[]{:S(2)}, u32[]{:S(2)}) collective-permute-start(f32[2,1,6,128]{3,2,1,0:T(8,128)S(1)} %get-tuple-element.60), channel_id=1, source_target_pairs={{8,0},{16,8},{24,16},{0,24},{9,1},{17,9},{25,17},{1,25},{10,2},{18... | collective-permute-start | bytes 18440 | tf_op jit(solution)/shard_map/ppermute | solution.py:31
  186.4 4.9 %collective-permute-start.22 = (f32[2,8,1,128]{3,2,1,0:T(1,128)S(1)}, f32[2,8,1,128]{3,2,1,0:T(1,128)S(1)}, u32[]{:S(2)}, u32[]{:S(2)}) collective-permute-start(f32[2,8,1,128]{3,2,1,0:T(1,128)S(1)} %get-tuple-element.43), channel_id=1, source_target_pairs={{0,1},{1,2},{2,3},{3,4},{4,5},{5,6},{6,7},{7,0},{8,9},{9,10},{10,1... | collective-permute-start | bytes 24584 | tf_op jit(solution)/shard_map/ppermute | solution.py:28
  186.5 4.9 %collective-permute-start.23 = (f32[2,8,1,128]{3,2,1,0:T(1,128)S(1)}, f32[2,8,1,128]{3,2,1,0:T(1,128)S(1)}, u32[]{:S(2)}, u32[]{:S(2)}) collective-permute-start(f32[2,8,1,128]{3,2,1,0:T(1,128)S(1)} %get-tuple-element.44), channel_id=1, source_target_pairs={{1,0},{2,1},{3,2},{4,3},{5,4},{6,5},{7,6},{0,7},{9,8},{10,9},{11,1... | collective-permute-start | bytes 24584 | tf_op jit(solution)/shard_map/ppermute | solution.py:31
  245.8 4.6 %collective-permute-start.24 = (f32[1,6,128]{2,1,0:T(8,128)S(1)}, f32[1,6,128]{2,1,0:T(8,128)S(1)}, u32[]{:S(2)}, u32[]{:S(2)}) collective-permute-start(f32[1,6,128]{2,1,0:T(8,128)S(1)} %get-tuple-element.83), channel_id=1, source_target_pairs={{0,8},{8,16},{16,24},{24,0},{1,9},{9,17},{17,25},{25,1},{2,10},{10... | collective-permute-start | bytes 9224 | tf_op jit(solution)/shard_map/ppermute | solution.py:28
  251.7 4.9 %collective-permute-start.26 = (f32[8,1,128]{2,1,0:T(1,128)S(1)}, f32[8,1,128]{2,1,0:T(1,128)S(1)}, u32[]{:S(2)}, u32[]{:S(2)}) collective-permute-start(f32[8,1,128]{2,1,0:T(1,128)S(1)} %get-tuple-element.75), channel_id=1, source_target_pairs={{0,1},{1,2},{2,3},{3,4},{4,5},{5,6},{6,7},{7,0},{8,9},{9,10},{10,1... | collective-permute-start | bytes 12296 | tf_op jit(solution)/shard_map/ppermute | solution.py:28
  251.8 4.9 %collective-permute-start.27 = (f32[8,1,128]{2,1,0:T(1,128)S(1)}, f32[8,1,128]{2,1,0:T(1,128)S(1)}, u32[]{:S(2)}, u32[]{:S(2)}) collective-permute-start(f32[8,1,128]{2,1,0:T(1,128)S(1)} %get-tuple-element.76), channel_id=1, source_target_pairs={{1,0},{2,1},{3,2},{4,3},{5,4},{6,5},{7,6},{0,7},{9,8},{10,9},{11,1... | collective-permute-start | bytes 12296 | tf_op jit(solution)/shard_map/ppermute | solution.py:31
  268.4 4.6 %collective-permute-start.28 = (f32[2,1,6,128]{3,2,1,0:T(8,128)S(1)}, f32[2,1,6,128]{3,2,1,0:T(8,128)S(1)}, u32[]{:S(2)}, u32[]{:S(2)}) collective-permute-start(f32[2,1,6,128]{3,2,1,0:T(8,128)S(1)} %get-tuple-element.57), channel_id=1, source_target_pairs={{0,8},{8,16},{16,24},{24,0},{1,9},{9,17},{17,25},{25,1},{2,10},{10... | collective-permute-start | bytes 18440 | tf_op jit(solution)/shard_map/ppermute | solution.py:28
  270.8 3.7 %collective-permute-start.29 = (f32[2,1,6,128]{3,2,1,0:T(8,128)S(1)}, f32[2,1,6,128]{3,2,1,0:T(8,128)S(1)}, u32[]{:S(2)}, u32[]{:S(2)}) collective-permute-start(f32[2,1,6,128]{3,2,1,0:T(8,128)S(1)} %get-tuple-element.58), channel_id=1, source_target_pairs={{8,0},{16,8},{24,16},{0,24},{9,1},{17,9},{25,17},{1,25},{10,2},{18... | collective-permute-start | bytes 18440 | tf_op jit(solution)/shard_map/ppermute | solution.py:31
  274.5 4.9 %collective-permute-start.30 = (f32[2,8,1,128]{3,2,1,0:T(1,128)S(1)}, f32[2,8,1,128]{3,2,1,0:T(1,128)S(1)}, u32[]{:S(2)}, u32[]{:S(2)}) collective-permute-start(f32[2,8,1,128]{3,2,1,0:T(1,128)S(1)} %get-tuple-element.41), channel_id=1, source_target_pairs={{0,1},{1,2},{2,3},{3,4},{4,5},{5,6},{6,7},{7,0},{8,9},{9,10},{10,1... | collective-permute-start | bytes 24584 | tf_op jit(solution)/shard_map/ppermute | solution.py:28
  274.5 4.9 %collective-permute-start.31 = (f32[2,8,1,128]{3,2,1,0:T(1,128)S(1)}, f32[2,8,1,128]{3,2,1,0:T(1,128)S(1)}, u32[]{:S(2)}, u32[]{:S(2)}) collective-permute-start(f32[2,8,1,128]{3,2,1,0:T(1,128)S(1)} %get-tuple-element.42), channel_id=1, source_target_pairs={{1,0},{2,1},{3,2},{4,3},{5,4},{6,5},{7,6},{0,7},{9,8},{10,9},{11,1... | collective-permute-start | bytes 24584 | tf_op jit(solution)/shard_map/ppermute | solution.py:31
  335.7 4.5 %collective-permute-start.32 = (f32[1,6,128]{2,1,0:T(8,128)S(1)}, f32[1,6,128]{2,1,0:T(8,128)S(1)}, u32[]{:S(2)}, u32[]{:S(2)}) collective-permute-start(f32[1,6,128]{2,1,0:T(8,128)S(1)} %get-tuple-element.81), channel_id=1, source_target_pairs={{0,8},{8,16},{16,24},{24,0},{1,9},{9,17},{17,25},{25,1},{2,10},{10... | collective-permute-start | bytes 9224 | tf_op jit(solution)/shard_map/ppermute | solution.py:28
  341.6 4.9 %collective-permute-start.34 = (f32[8,1,128]{2,1,0:T(1,128)S(1)}, f32[8,1,128]{2,1,0:T(1,128)S(1)}, u32[]{:S(2)}, u32[]{:S(2)}) collective-permute-start(f32[8,1,128]{2,1,0:T(1,128)S(1)} %get-tuple-element.73), channel_id=1, source_target_pairs={{0,1},{1,2},{2,3},{3,4},{4,5},{5,6},{6,7},{7,0},{8,9},{9,10},{10,1... | collective-permute-start | bytes 12296 | tf_op jit(solution)/shard_map/ppermute | solution.py:28
  341.7 4.9 %collective-permute-start.35 = (f32[8,1,128]{2,1,0:T(1,128)S(1)}, f32[8,1,128]{2,1,0:T(1,128)S(1)}, u32[]{:S(2)}, u32[]{:S(2)}) collective-permute-start(f32[8,1,128]{2,1,0:T(1,128)S(1)} %get-tuple-element.74), channel_id=1, source_target_pairs={{1,0},{2,1},{3,2},{4,3},{5,4},{6,5},{7,6},{0,7},{9,8},{10,9},{11,1... | collective-permute-start | bytes 12296 | tf_op jit(solution)/shard_map/ppermute | solution.py:31
  (12 other events, 191.9 us)

commit v2 on v1

v2 whole, which is shorter than its diff:
```python
import functools

import jax
import jax.numpy as jnp
from jax import lax
from jax.experimental import pallas as pl
from jax.experimental.pallas import tpu as pltpu
from jax.sharding import PartitionSpec as P

ITERS = 4


TIME_STEP = 0.05
KERNEL_NORM = 4.0 / (3.141592653589793 * 64.0)
REST_LIGHT = 1.2
REST_HEAVY = 1.5
STIFF_LIGHT = 100.0
STIFF_HEAVY = 200.0
MASS_LIGHT = 1.0
MASS_HEAVY = 1.5
SENTINEL = 1e30


EMPTY = -1e30
FAR = 1e30
LIMIT = 1e29
DIRS = tuple((dx, dy) for dx in (-1, 0, 1) for dy in (-1, 0, 1) if dx or dy)


def split3(value):
    high = value.astype(jnp.bfloat16).astype(jnp.float32)
    rest = value - high
    mid = rest.astype(jnp.bfloat16).astype(jnp.float32)
    low = (rest - mid).astype(jnp.bfloat16).astype(jnp.float32)
    return high, mid, low


def put_rows(ref, row, values, width):
    for at, value in enumerate(values):
        ref[row, at * width : (at + 1) * width, :] = value


def source_features(x, y, live, jf, row, width):
    x = jnp.where(live, x - 0.5, 0.0)
    y = jnp.where(live, y - 0.5, 0.0)
    xh, xm, xl = split3(x)
    yh, ym, yl = split3(y)
    bh, bm, bl = split3(jnp.where(live, -(x * x + y * y), EMPTY))
    one = jnp.ones_like(x)
    nil = jnp.zeros_like(x)
    put_rows(
        jf,
        row,
        [xh, xh, xm, xh, xl, xm, bh, bm, yh, yh, ym, yh, yl, ym, bl, nil]
        + [one, one, one, nil, nil, nil, nil, nil],
        width,
    )


def pair_features(jf, lhs, row, width, half):
    for n in range(width - half):
        first = jf[row, pl.ds(n, 24, stride=width), :]
        second = jf[row, pl.ds(n + half, 24, stride=width), :]
        both = jnp.concatenate([first, second], axis=0)
        lhs[row, n] = both.T.astype(jnp.bfloat16)


def target_features(x, y, xf, yf, af, row, width):
    x = jnp.where(x < LIMIT, x, 0.0) - 0.5
    y = y - 0.5
    one = jnp.ones_like(x)
    nil = jnp.zeros_like(x)
    for at in range(3):
        h, m, l = split3(2.0 * (x - (at - 1.0)))
        put_rows(xf.at[row], at, [h, m, h, l, h, m, one, one], width)
        h, m, l = split3(2.0 * (y - (at - 1.0)))
        put_rows(yf.at[row], at, [h, m, h, l, h, m, one, nil], width)
    for ax in range(3):
        for ay in range(3):
            dx = x - (ax - 1.0)
            dy = y - (ay - 1.0)
            h, m, l = split3(1.0 - (dx * dx + dy * dy))
            put_rows(af.at[row], 3 * ax + ay, [h, m, l, nil, nil, nil, nil, nil], width)


def target_block(xf, yf, af, row, cell, ax, ay, width):
    return jnp.concatenate(
        [
            xf[row, ax, pl.ds(cell + 1, 8, stride=width), :],
            yf[row, ay, pl.ds(cell + 1, 8, stride=width), :],
            af[row, 3 * ax + ay, pl.ds(cell + 1, 8, stride=width), :],
        ],
        axis=0,
    )


def overlap(lhs, xf, yf, af, row, cell, ax, ay, width, half):
    first = target_block(xf, yf, af, row, cell, ax, ay, width)
    second = target_block(xf, yf, af, row, cell + half, ax, ay, width)
    nil = jnp.zeros_like(first)
    rhs = jnp.concatenate(
        [
            jnp.concatenate([first, nil], axis=1),
            jnp.concatenate([nil, second], axis=1),
        ],
        axis=0,
    ).astype(jnp.bfloat16)
    raw = jnp.dot(lhs[row + ax, cell + ay], rhs, preferred_element_type=jnp.float32)
    return jnp.maximum(raw, 0.0)


def all_features(pos, jf, lhs, xf, yf, af, rows, width, half):
    def source_row(row, carry):
        source_features(pos[0, row], pos[1, row], pos[0, row] < LIMIT, jf, row, width)
        pair_features(jf, lhs, row, width, half)
        return carry

    lax.fori_loop(0, rows + 2, source_row, 0)

    def target_row(row, carry):
        target_features(pos[0, row + 1], pos[1, row + 1], xf, yf, af, row, width)
        return carry

    lax.fori_loop(0, rows, target_row, 0)


def value_rows(x, y, term, live, vf, row, width):
    x = jnp.where(live, x - 0.5, 0.0)
    y = jnp.where(live, y - 0.5, 0.0)
    term = jnp.where(live, term, 0.0)
    highs, mids = [], []
    for value in (jnp.ones_like(x), x, y, term, term * x, term * y):
        high, mid, _ = split3(value)
        highs.append(high)
        mids.append(mid)
    nil = jnp.zeros_like(x)
    put_rows(vf, row, highs + [nil, nil] + mids + [nil, nil], width)


def density_row(lhs, xf, yf, af, dens, ghi, glo, row, cols, slots):
    width, half = cols + 2, cols // 2
    for cell in range(half):
        total = jnp.zeros((8, 2 * slots), jnp.float32)
        for ax in range(3):
            for ay in range(3):
                w = overlap(lhs, xf, yf, af, row, cell, ax, ay, width, half)
                square = w * w
                high = square.astype(jnp.bfloat16)
                ghi[row, cell, 3 * ax + ay] = high
                glo[row, cell, 3 * ax + ay] = (square - high.astype(jnp.float32)).astype(
                    jnp.bfloat16
                )
                total = total + jnp.sum(
                    (square * w).reshape(slots // 8, 8, 2 * slots), axis=0
                )
        got = jnp.sum(total, axis=0, keepdims=True)
        dens[row, cell + 1 : cell + 2, :] = got[:, :slots]
        dens[row, cell + half + 1 : cell + half + 2, :] = got[:, slots:]


def force_row(vf, ghi, glo, sums, row, cols, slots):
    width, half = cols + 2, cols // 2
    for cell in range(half):
        zero = jnp.zeros((8, slots), jnp.float32)
        parts = [[zero, zero, zero], [zero, zero, zero]]
        for ax in range(3):
            for ay in range(3):
                value = jnp.concatenate(
                    [
                        vf[row + ax, pl.ds(cell + ay, 16, stride=width), :],
                        vf[row + ax, pl.ds(cell + ay + half, 16, stride=width), :],
                    ],
                    axis=0,
                ).astype(jnp.bfloat16)
                got = jnp.dot(
                    value, ghi[row, cell, 3 * ax + ay], preferred_element_type=jnp.float32
                ) + jnp.dot(
                    value, glo[row, cell, 3 * ax + ay], preferred_element_type=jnp.float32
                )
                pieces = (
                    got[0:8, :slots] + got[8:16, :slots],
                    got[16:24, slots:] + got[24:32, slots:],
                )
                for acc, piece in zip(parts, pieces):
                    acc[0] = acc[0] + piece
                    if ax != 1:
                        acc[1] = acc[1] + piece if ax == 2 else acc[1] - piece
                    if ay != 1:
                        acc[2] = acc[2] + piece if ay == 2 else acc[2] - piece
        for at, acc in zip((cell, cell + half), parts):
            plain, by_x, by_y = acc
            rows_out = (
                plain[0:1],
                plain[1:2] + by_x[0:1],
                plain[2:3] + by_y[0:1],
                plain[3:4],
                plain[4:5] + by_x[3:4],
                plain[5:6] + by_y[3:4],
            )
            for k, value in enumerate(rows_out):
                sums[k, at + 1 : at + 2, :] = value


def remote(src, dst, send, recv, to_x, to_y):
    return pltpu.make_async_remote_copy(
        src_ref=src,
        dst_ref=dst,
        send_sem=send,
        recv_sem=recv,
        device_id=(to_x, to_y),
        device_id_type=pl.DeviceIdType.MESH,
    )


def pack_edges(field, out, par, count, rows, cols):
    for d, (dx, dy) in enumerate(DIRS):
        row = rows if dx > 0 else 1
        cell = cols if dy > 0 else 1
        for k in range(count):
            if dy == 0:
                out[par, d, k, : cols + 2, :] = field[k, row]
            elif dx == 0:
                for r in range(1, rows + 1):
                    out[par, d, k, r : r + 1, :] = field[k, r, cell : cell + 1, :]
            else:
                out[par, d, k, 0:1, :] = field[k, row, cell : cell + 1, :]


def unpack_edges(field, got, par, count, rows, cols):
    for d, (dx, dy) in enumerate(DIRS):
        row = 0 if dx > 0 else rows + 1
        cell = 0 if dy > 0 else cols + 1
        for k in range(count):
            if dy == 0:
                field[k, row, 1 : cols + 1, :] = got[par, d, k, 1 : cols + 1, :]
            elif dx == 0:
                for r in range(1, rows + 1):
                    field[k, r, cell : cell + 1, :] = got[par, d, k, r : r + 1, :]
            else:
                field[k, row, cell : cell + 1, :] = got[par, d, k, 0:1, :]


def step_kernel(
    nx, ny,
    pos_in, vel_in, oth_in, code_in,
    pos_out, vel_out, press_out, bounds_out,
    base, pos, acc, press, parts, ratio, dens,
    jf, lhs, xf, yf, af, vf, sums, ghi, glo,
    pos_snd, pos_rcv, ab_snd, ab_rcv, one_snd, one_rcv, two_snd, two_rcv,
    pos_ss, pos_rs, ab_ss, ab_rs, one_ss, one_rs, two_ss, two_rs,
):
    _, rows, cols, slots = pos_in.shape
    width, half = cols + 2, cols // 2
    me_x, me_y = lax.axis_index("gx"), lax.axis_index("gy")

    def at_x(step):
        return lax.rem(me_x + step + nx, nx)

    def at_y(step):
        return lax.rem(me_y + step + ny, ny)

    barrier = pltpu.get_barrier_semaphore()
    partners = [(0, k) for k in range(1, ny)] + [(k, 0) for k in range(1, nx)]
    partners += [(dx, dy) for dx, dy in DIRS if dx and dy]
    for dx, dy in partners:
        pl.semaphore_signal(
            barrier, inc=1, device_id=(at_x(dx), at_y(dy)), device_id_type=pl.DeviceIdType.MESH
        )

    for ref in (base, acc, press, ratio, dens, sums, parts, pos):
        ref[...] = jnp.zeros_like(ref)
    for ref in (pos_snd, ab_snd):
        ref[...] = jnp.zeros_like(ref)
    for row in range(rows):
        for k, source in enumerate((pos_in, vel_in, oth_in)):
            for c in range(2):
                base[2 * k + c, row, 1 : cols + 1, :] = source[c, row]
        base[6, row, 1 : cols + 1, :] = code_in[row]
    pl.semaphore_wait(barrier, len(partners))

    def halo(src, dst, send, recv, par):
        return [
            remote(src.at[par, d], dst.at[par, d], send.at[par, d], recv.at[par, d], at_x(dx), at_y(dy))
            for d, (dx, dy) in enumerate(DIRS)
        ]

    def one_iteration(it, carry):
        par = lax.rem(it, 2)

        def predict(row, carry):
            live = base[6, row] > 0
            for c in range(2):
                vel = base[2 + c, row] + TIME_STEP * (base[4 + c, row] + acc[c, row])
                moved = base[c, row] + TIME_STEP * vel
                pos[c, row + 1] = jnp.where(live, moved, FAR if c == 0 else 0.0)
            return carry

        lax.fori_loop(0, rows, predict, 0)
        pack_edges(pos, pos_snd, par, 2, rows, cols)
        copies = halo(pos_snd, pos_rcv, pos_ss, pos_rs, par)
        for copy in copies:
            copy.start()
        for copy in copies:
            copy.wait()
        unpack_edges(pos, pos_rcv, par, 2, rows, cols)

        all_features(pos, jf, lhs, xf, yf, af, rows, width, half)

        def density_step(row, carry):
            density_row(lhs, xf, yf, af, dens, ghi, glo, row, cols, slots)
            return carry

        lax.fori_loop(0, rows, density_step, 0)

        def bounds_step(row, carry):
            code = base[6, row]
            live = code > 0.5
            heavy = code > 1.5
            density = KERNEL_NORM * dens[row]
            own = density / jnp.where(heavy, REST_HEAVY, REST_LIGHT)
            ratio[row] = own
            safe = jnp.where(live, density, 1.0)
            alpha = jnp.where(live, press[row] / (safe * safe), 0.0)
            stiff = jnp.where(heavy, STIFF_HEAVY, STIFF_LIGHT)
            beta = jnp.where(live, stiff * (own - 1.0) / (safe * safe), 0.0)
            parts[0, row + 1] = alpha
            parts[1, row + 1] = jnp.where(heavy, 0.0, beta)
            parts[2, row + 1] = jnp.where(heavy, beta, 0.0)
            light_sel = live & jnp.logical_not(heavy)
            heavy_sel = live & heavy
            return (
                jnp.maximum(carry[0], jnp.where(light_sel, own, -SENTINEL)),
                jnp.maximum(carry[1], jnp.where(heavy_sel, own, -SENTINEL)),
                jnp.maximum(carry[2], jnp.where(light_sel, -own, -SENTINEL)),
                jnp.maximum(carry[3], jnp.where(heavy_sel, -own, -SENTINEL)),
            )

        floor = jnp.full((width, slots), -SENTINEL, jnp.float32)
        local = lax.fori_loop(0, rows, bounds_step, (floor,) * 4)
        for k, value in enumerate(local):
            one_snd[par, k : k + 1, :] = jnp.max(value, axis=0, keepdims=True)
        one_snd[par, 4:8, :] = jnp.full((4, slots), -SENTINEL, jnp.float32)
        firsts = [
            remote(one_snd.at[par], one_rcv.at[par, k], one_ss.at[par, k], one_rs.at[par, k], me_x, at_y(k))
            for k in range(1, ny)
        ]
        for copy in firsts:
            copy.start()
        pack_edges(parts, ab_snd, par, 3, rows, cols)
        copies = halo(ab_snd, ab_rcv, ab_ss, ab_rs, par)
        for copy in copies:
            copy.start()
        for copy in firsts:
            copy.wait()
        best = one_snd[par]
        for k in range(1, ny):
            best = jnp.maximum(best, one_rcv[par, k])
        two_snd[par] = best
        seconds = [
            remote(two_snd.at[par], two_rcv.at[par, k], two_ss.at[par, k], two_rs.at[par, k], at_x(k), me_y)
            for k in range(1, nx)
        ]
        for copy in seconds:
            copy.start()
        for copy in copies:
            copy.wait()
        unpack_edges(parts, ab_rcv, par, 3, rows, cols)
        for copy in seconds:
            copy.wait()
        for k in range(1, nx):
            best = jnp.maximum(best, two_rcv[par, k])
        bound = jnp.max(best, axis=1, keepdims=True)
        bounds_out[it] = jnp.broadcast_to(bound, (8, slots))
        relax = 1.0 / (1.0 + bound[0:2] + bound[2:4])
        relax_light = relax[0:1]
        relax_heavy = relax[1:2]

        def term_step(row, carry):
            term = parts[0, row] + relax_light * parts[1, row] + relax_heavy * parts[2, row]
            value_rows(pos[0, row], pos[1, row], term, pos[0, row] < LIMIT, vf, row, width)
            return carry

        lax.fori_loop(0, rows + 2, term_step, 0)

        def force_step(row, carry):
            force_row(vf, ghi, glo, sums, row, cols, slots)
            code = base[6, row]
            live = code > 0.5
            heavy = code > 1.5
            relaxed = jnp.where(heavy, STIFF_HEAVY * relax_heavy, STIFF_LIGHT * relax_light)
            press[row] = jnp.where(live, press[row] + relaxed * (ratio[row] - 1.0), 0.0)
            term = (
                parts[0, row + 1]
                + relax_light * parts[1, row + 1]
                + relax_heavy * parts[2, row + 1]
            )
            scale = jnp.where(
                heavy, 6.0 * KERNEL_NORM / MASS_HEAVY, 6.0 * KERNEL_NORM / MASS_LIGHT
            )
            for c in range(2):
                own = pos[c, row + 1] - 0.5
                force = term * (own * sums[0] - sums[1 + c]) + own * sums[3] - sums[4 + c]
                acc[c, row] = jnp.where(live, scale * force, 0.0)
            return carry

        lax.fori_loop(0, rows, force_step, 0)
        return carry

    lax.fori_loop(0, ITERS, one_iteration, 0)

    def finish(row, carry):
        live = base[6, row] > 0.5
        press_out[row] = press[row, 1 : cols + 1, :]
        for c in range(2):
            vel = base[2 + c, row] + TIME_STEP * (base[4 + c, row] + acc[c, row])
            vel = jnp.where(live, vel, 0.0)
            place = jnp.where(live, base[c, row] + TIME_STEP * vel, 0.0)
            vel_out[c, row] = vel[1 : cols + 1]
            pos_out[c, row] = place[1 : cols + 1]
        return carry

    lax.fori_loop(0, rows, finish, 0)


def local(position, velocity, other_accel, phase_ids, counts):
    rows, cols, slots = phase_ids.shape
    width, half = cols + 2, cols // 2
    nx, ny = lax.axis_size("gx"), lax.axis_size("gy")
    high = max(width, rows + 2)
    slot_index = jnp.arange(slots, dtype=jnp.int32)
    live = slot_index[None, None, :] < counts[:, :, None]
    codes = jnp.where(live, phase_ids + 1, 0).astype(jnp.float32)

    def vm(*shape):
        return pltpu.VMEM(shape, jnp.float32)

    def half_vm(*shape):
        return pltpu.VMEM(shape, jnp.bfloat16)

    dma = pltpu.SemaphoreType.DMA
    new_pos, new_vel, pressure, bounds = pl.pallas_call(
        functools.partial(step_kernel, nx, ny),
        out_shape=(
            jax.ShapeDtypeStruct((2, rows, cols, slots), jnp.float32),
            jax.ShapeDtypeStruct((2, rows, cols, slots), jnp.float32),
            jax.ShapeDtypeStruct((rows, cols, slots), jnp.float32),
            jax.ShapeDtypeStruct((ITERS, 8, slots), jnp.float32),
        ),
        in_specs=[pl.BlockSpec(memory_space=pltpu.VMEM)] * 4,
        out_specs=(pl.BlockSpec(memory_space=pltpu.VMEM),) * 4,
        scratch_shapes=[
            vm(7, rows, width, slots),
            vm(2, rows + 2, width, slots),
            vm(2, rows, width, slots),
            vm(rows, width, slots),
            vm(3, rows + 2, width, slots),
            vm(rows, width, slots),
            vm(rows, width, slots),
            vm(rows + 2, 24 * width, slots),
            half_vm(rows + 2, width - half, slots, 48),
            vm(rows, 3, 8 * width, slots),
            vm(rows, 3, 8 * width, slots),
            vm(rows, 9, 8 * width, slots),
            vm(rows + 2, 16 * width, slots),
            vm(6, width, slots),
            half_vm(rows, half, 9, slots, 2 * slots),
            half_vm(rows, half, 9, slots, 2 * slots),
            vm(2, 8, 2, high, slots),
            vm(2, 8, 2, high, slots),
            vm(2, 8, 3, high, slots),
            vm(2, 8, 3, high, slots),
            vm(2, 8, slots),
            vm(2, ny, 8, slots),
            vm(2, 8, slots),
            vm(2, nx, 8, slots),
            dma((2, 8)), dma((2, 8)), dma((2, 8)), dma((2, 8)),
            dma((2, ny)), dma((2, ny)), dma((2, nx)), dma((2, nx)),
        ],
        compiler_params=pltpu.CompilerParams(collective_id=0, has_side_effects=True),
    )(position, velocity, other_accel, codes)
    tops = bounds[:, :2, 0]
    lows = -bounds[:, 2:4, 0]
    return new_pos, new_vel, pressure, jnp.concatenate([tops, lows], axis=1)


def solution(mesh):
    placed = (
        P(None, "gx", "gy", None),
        P(None, "gx", "gy", None),
        P(None, "gx", "gy", None),
        P("gx", "gy", None),
        P("gx", "gy"),
    )
    return jax.shard_map(
        local,
        mesh=mesh,
        in_specs=placed,
        out_specs=(P(None, "gx", "gy", None), P(None, "gx", "gy", None), P("gx", "gy", None), P()),
        check_vma=False,
    )
```

time: 361 us -> 110 us (0.30)
  blocking collectives: 154 us -> 0 us
  starting transfers between devices: 60.1 us -> 0 us
  other arithmetic: 41.1 us -> 1.44 us
  Pallas kernels: 68 us -> 101 us
  waiting for transfers between devices: 30.4 us -> 0 us
    pmax x4 -> x0, blocking collectives: 154 us -> none  [global_bounds(): bounds = lax.pmax(jnp.concatenate([top_local, -low_local]), ('gx', 'gy'))]
    ppermute x36 -> x0, starting transfers between devices: 60.1 us -> none  [the longest x18 39 us: padded(): lax.ppermute(lax.slice_in_dim(block, 0, width, axis=dim), axis, backward)]
    pallas_call x8 -> x1, Pallas kernels: 68 us -> 101 us  [local(): pl.pallas_call(functools.partial(step_kernel, nx, ny), out_shape=(jax.Sha...]
    ppermute x36 -> x0, waiting for transfers between devices: 30.4 us -> none  [the longest x18 20.2 us: padded(): lax.ppermute(lax.slice_in_dim(block, block.shape[dim] - width, None, axis...]
    select_n x5 -> x0, other arithmetic: 13.6 us -> none  [the longest x4 13.5 us: pressure_update(): jnp.where(live_bool, pressure / (safe_density * safe_density), 0.0)]
    concatenate x12 -> x1, other arithmetic: 10.6 us -> 0.01 us  [local(): return (new_pos, new_vel, pressure, jnp.concatenate([tops, lows], axis=1))]
    reduce_max x4 -> x0, other arithmetic: 5.86 us -> none  [global_bounds(): jnp.max(jnp.where(light_sel, density_ratio, -SENTINEL))]
    neg x4 -> x0, other arithmetic: 5.72 us -> none  [global_bounds(): bounds = lax.pmax(jnp.concatenate([top_local, -low_local]), ('gx', 'gy'))]
  transfers between devices with their start and end apart: 36 -> 0, of which waited for: 22 -> 0; matrix products, arithmetic and copies ran while one was open for 0% -> 0% of each run, Pallas kernels for 0% -> 0%
where the time goes in v2:
time: 110 us; the launch traced here: 109 us
  Pallas kernels  101 us (92%)
  local copies, waits for them, and re-layouts  5.84 us (5%)
  other arithmetic  1.44 us (1%)
    pallas_call x1, Pallas kernels, local(): pl.pallas_call(functools.partial(step_kernel, nx, ny), out_shape=(jax.Sha...  101 us
    unnamed x19, local copies, waits for them, and re-layouts  5.64 us

profile of v2, /device:TPU:0, one launch (start us, length us, event | category | flops | bytes accessed | tf_op | source)
XLA Modules:
  0.0 109.3 jit_solution(10360887232802700601)
XLA Ops:
  0.6 0.0 copy-start.1
  0.6 1.4 %select_convert_fusion.code_in = f32[6,6,128]{2,1,0:T(8,128)} fusion(s32[6,6,128]{2,1,0:T(8,128)} %param.8, s32[6,6]{1,0:T(8,128)} %param.9), kind=kLoop, calls=%fused_computation | loop fusion | flops 18432 | bytes 37008 | tf_op jit(solution)/shard_map/convert_element_type | solution.py:432
  2.1 0.0 copy-done.1
  2.1 0.0 copy-start.2
  2.1 0.6 copy.17.pos_in
  2.7 0.1 copy-done.2
  2.8 0.0 copy-start.3
  2.8 0.6 copy.18.vel_in
  3.5 0.1 copy-done.3
  3.6 0.6 copy.19.oth_in
  4.2 101.3 %shard_map.84 = (f32[2,6,6,128]{3,2,1,0:T(8,128)}, f32[2,6,6,128]{3,2,1,0:T(8,128)}, f32[6,6,128]{2,1,0:T(8,128)}, f32[4,8,128]{2,1,0:T(8,128)}) custom-call(f32[2,6,6,128]{3,2,1,0:T(8,128)} %copy.17.pos_in, f32[2,6,6,128]{3,2,1,0:T(8,128)} %copy.18.vel_in, f32[2,6,6,128]{3,2,1,0:T(8,128)} %copy.19.oth_in, f32[6,6,128]{2,1,0:T(8,128)} %select_convert_fusion.code_in), custom_call_target="tpu_custom_call" | custom-call | tf_op jit(solution)/shard_map/pallas_call | solution.py:441
  105.6 0.0 copy-start.5
  105.6 0.0 copy-start
  105.6 1.5 %copy.22 = f32[2,6,6,128]{3,0,2,1:T(2,128)} copy(f32[2,6,6,128]{3,2,1,0:T(8,128)} %get-tuple-element.16) | data formatting | bytes 73728
  107.1 0.0 copy-done.5
  107.1 0.1 copy.20
  107.2 0.1 copy.21
  107.3 0.7 copy.24
  107.9 0.0 copy-done
  108.0 0.0 copy-start.4
  108.0 0.6 copy.23
  108.6 0.1 copy-done.4
  108.7 0.6 copy.26
  (2 shorter events, 0.0 us)
Async XLA Ops:
  0.6 1.4 %copy-start.1 = (f32[2,6,6,128]{3,0,2,1:T(2,128)S(1)}, f32[2,6,6,128]{3,0,2,1:T(2,128)}, u32[]{:S(2)}) copy-start(f32[2,6,6,128]{3,0,2,1:T(2,128)} %param.5) | copy-start | bytes 110596
  2.1 0.8 copy-start.2
  2.8 0.8 copy-start.3
  105.6 1.5 %copy-start.5 = (f32[4,8,128]{2,1,0:T(8,128)S(1)}, f32[4,8,128]{2,1,0:T(8,128)}, u32[]{:S(2)}) copy-start(f32[4,8,128]{2,1,0:T(8,128)} %get-tuple-element.11) | copy-start | bytes 49156
  105.6 2.4 %copy-start = (f32[2,6,6,128]{3,2,1,0:T(8,128)S(1)}, f32[2,6,6,128]{3,2,1,0:T(8,128)}, u32[]{:S(2)}) copy-start(f32[2,6,6,128]{3,2,1,0:T(8,128)} %get-tuple-element.17) | copy-start | bytes 110596
  108.0 0.7 copy-start.4

commit v3 on v2

--- a/solution.py
+++ b/solution.py
@@ -109,7 +109,7 @@
     return jnp.maximum(raw, 0.0)
 
 
-def all_features(pos, jf, lhs, xf, yf, af, rows, width, half):
+def all_sources(pos, jf, lhs, rows, width, half):
     def source_row(row, carry):
         source_features(pos[0, row], pos[1, row], pos[0, row] < LIMIT, jf, row, width)
         pair_features(jf, lhs, row, width, half)
@@ -117,6 +117,8 @@
 
     lax.fori_loop(0, rows + 2, source_row, 0)
 
+
+def all_targets(pos, xf, yf, af, rows, width):
     def target_row(row, carry):
         target_features(pos[0, row + 1], pos[1, row + 1], xf, yf, af, row, width)
         return carry
@@ -137,7 +139,7 @@
     put_rows(vf, row, highs + [nil, nil] + mids + [nil, nil], width)
 
 
-def density_row(lhs, xf, yf, af, dens, ghi, glo, row, cols, slots):
+def density_row(lhs, xf, yf, af, dens, gain, row, cols, slots):
     width, half = cols + 2, cols // 2
     for cell in range(half):
         total = jnp.zeros((8, 2 * slots), jnp.float32)
@@ -146,10 +148,10 @@
                 w = overlap(lhs, xf, yf, af, row, cell, ax, ay, width, half)
                 square = w * w
                 high = square.astype(jnp.bfloat16)
-                ghi[row, cell, 3 * ax + ay] = high
-                glo[row, cell, 3 * ax + ay] = (square - high.astype(jnp.float32)).astype(
-                    jnp.bfloat16
-                )
+                gain[row, cell, 3 * ax + ay, :slots, :] = high
+                gain[row, cell, 3 * ax + ay, slots:, :] = (
+                    square - high.astype(jnp.float32)
+                ).astype(jnp.bfloat16)
                 total = total + jnp.sum(
                     (square * w).reshape(slots // 8, 8, 2 * slots), axis=0
                 )
@@ -158,7 +160,7 @@
         dens[row, cell + half + 1 : cell + half + 2, :] = got[:, slots:]
 
 
-def force_row(vf, ghi, glo, sums, row, cols, slots):
+def force_row(vf, gain, sums, row, cols, slots):
     width, half = cols + 2, cols // 2
     for cell in range(half):
         zero = jnp.zeros((8, slots), jnp.float32)
@@ -173,9 +175,9 @@
                     axis=0,
                 ).astype(jnp.bfloat16)
                 got = jnp.dot(
-                    value, ghi[row, cell, 3 * ax + ay], preferred_element_type=jnp.float32
-                ) + jnp.dot(
-                    value, glo[row, cell, 3 * ax + ay], preferred_element_type=jnp.float32
+                    jnp.concatenate([value, value], axis=1),
+                    gain[row, cell, 3 * ax + ay],
+                    preferred_element_type=jnp.float32,
                 )
                 pieces = (
                     got[0:8, :slots] + got[8:16, :slots],
@@ -245,7 +247,7 @@
     pos_in, vel_in, oth_in, code_in,
     pos_out, vel_out, press_out, bounds_out,
     base, pos, acc, press, parts, ratio, dens,
-    jf, lhs, xf, yf, af, vf, sums, ghi, glo,
+    jf, lhs, xf, yf, af, vf, sums, gain,
     pos_snd, pos_rcv, ab_snd, ab_rcv, one_snd, one_rcv, two_snd, two_rcv,
     pos_ss, pos_rs, ab_ss, ab_rs, one_ss, one_rs, two_ss, two_rs,
 ):
@@ -300,14 +302,15 @@
         copies = halo(pos_snd, pos_rcv, pos_ss, pos_rs, par)
         for copy in copies:
             copy.start()
+        all_targets(pos, xf, yf, af, rows, width)
         for copy in copies:
             copy.wait()
         unpack_edges(pos, pos_rcv, par, 2, rows, cols)
 
-        all_features(pos, jf, lhs, xf, yf, af, rows, width, half)
+        all_sources(pos, jf, lhs, rows, width, half)
 
         def density_step(row, carry):
-            density_row(lhs, xf, yf, af, dens, ghi, glo, row, cols, slots)
+            density_row(lhs, xf, yf, af, dens, gain, row, cols, slots)
             return carry
 
         lax.fori_loop(0, rows, density_step, 0)
@@ -383,7 +386,7 @@
         lax.fori_loop(0, rows + 2, term_step, 0)
 
         def force_step(row, carry):
-            force_row(vf, ghi, glo, sums, row, cols, slots)
+            force_row(vf, gain, sums, row, cols, slots)
             code = base[6, row]
             live = code > 0.5
             heavy = code > 1.5
@@ -463,8 +466,7 @@
             vm(rows, 9, 8 * width, slots),
             vm(rows + 2, 16 * width, slots),
             vm(6, width, slots),
-            half_vm(rows, half, 9, slots, 2 * slots),
-            half_vm(rows, half, 9, slots, 2 * slots),
+            half_vm(rows, half, 9, 2 * slots, 2 * slots),
             vm(2, 8, 2, high, slots),
             vm(2, 8, 2, high, slots),
             vm(2, 8, 3, high, slots),

time: 110 us -> 112 us (1.018)
  Pallas kernels: 101 us -> 104 us
    pallas_call x1, Pallas kernels: 101 us -> 104 us  [local(): pl.pallas_call(functools.partial(step_kernel, nx, ny), out_shape=(jax.Sha...]
where the time goes in v3:
time: 112 us
  Pallas kernels  104 us (93%)
  local copies, waits for them, and re-layouts  5.84 us (5%)
  other arithmetic  1.44 us (1%)
    pallas_call x1, Pallas kernels, local(): pl.pallas_call(functools.partial(step_kernel, nx, ny), out_shape=(jax.Sha...  104 us
    unnamed x19, local copies, waits for them, and re-layouts  5.64 us

profile of v3, /device:TPU:0, one launch (start us, length us, event | category | flops | bytes accessed | tf_op | source)
XLA Modules:
  0.0 111.7 jit_solution(11999224061761032652)
XLA Ops:
  0.6 0.0 copy-start.1
  0.6 1.4 %select_convert_fusion.code_in = f32[6,6,128]{2,1,0:T(8,128)} fusion(s32[6,6,128]{2,1,0:T(8,128)} %param.8, s32[6,6]{1,0:T(8,128)} %param.9), kind=kLoop, calls=%fused_computation | loop fusion | flops 18432 | bytes 37008 | tf_op jit(solution)/shard_map/convert_element_type | solution.py:435
  2.1 0.0 copy-done.1
  2.1 0.0 copy-start.2
  2.1 0.6 copy.17.pos_in
  2.7 0.1 copy-done.2
  2.8 0.0 copy-start.3
  2.8 0.6 copy.18.vel_in
  3.5 0.1 copy-done.3
  3.6 0.6 copy.19.oth_in
  4.2 103.7 %shard_map.84 = (f32[2,6,6,128]{3,2,1,0:T(8,128)}, f32[2,6,6,128]{3,2,1,0:T(8,128)}, f32[6,6,128]{2,1,0:T(8,128)}, f32[4,8,128]{2,1,0:T(8,128)}) custom-call(f32[2,6,6,128]{3,2,1,0:T(8,128)} %copy.17.pos_in, f32[2,6,6,128]{3,2,1,0:T(8,128)} %copy.18.vel_in, f32[2,6,6,128]{3,2,1,0:T(8,128)} %copy.19.oth_in, f32[6,6,128]{2,1,0:T(8,128)} %select_convert_fusion.code_in), custom_call_target="tpu_custom_call" | custom-call | tf_op jit(solution)/shard_map/pallas_call | solution.py:444
  107.9 0.0 copy-start.5
  108.0 0.0 copy-start
  108.0 1.5 %copy.22 = f32[2,6,6,128]{3,0,2,1:T(2,128)} copy(f32[2,6,6,128]{3,2,1,0:T(8,128)} %get-tuple-element.16) | data formatting | bytes 73728
  109.4 0.0 copy-done.5
  109.4 0.1 copy.20
  109.5 0.1 copy.21
  109.6 0.7 copy.24
  110.3 0.0 copy-done
  110.3 0.0 copy-start.4
  110.3 0.6 copy.23
  110.9 0.1 copy-done.4
  111.0 0.6 copy.26
  (2 shorter events, 0.0 us)
Async XLA Ops:
  0.6 1.4 %copy-start.1 = (f32[2,6,6,128]{3,0,2,1:T(2,128)S(1)}, f32[2,6,6,128]{3,0,2,1:T(2,128)}, u32[]{:S(2)}) copy-start(f32[2,6,6,128]{3,0,2,1:T(2,128)} %param.5) | copy-start | bytes 110596
  2.1 0.8 copy-start.2
  2.8 0.8 copy-start.3
  107.9 1.5 %copy-start.5 = (f32[4,8,128]{2,1,0:T(8,128)S(1)}, f32[4,8,128]{2,1,0:T(8,128)}, u32[]{:S(2)}) copy-start(f32[4,8,128]{2,1,0:T(8,128)} %get-tuple-element.11) | copy-start | bytes 49156
  108.0 2.4 %copy-start = (f32[2,6,6,128]{3,2,1,0:T(8,128)S(1)}, f32[2,6,6,128]{3,2,1,0:T(8,128)}, u32[]{:S(2)}) copy-start(f32[2,6,6,128]{3,2,1,0:T(8,128)} %get-tuple-element.17) | copy-start | bytes 110596
  110.3 0.7 copy-start.4
